TPU v7x, 256 devices: a whole 4x4x8 slice. The times are simulated.
256 devices in a mesh: seq: 32 (over z, y), head: 8 (over x, core).
Axes of the slice: x: 4, y: 4, z: 8, core: 2. Of those that a mesh axis runs over, the one named last changes fastest.
Arguments:
- queries: bfloat16 [32768, 12288], P(('seq', 'head')), may hold values from -8 to 8
- latent: bfloat16 [32768, 512], P(('seq', 'head')), may hold values from -6 to 6
- rope_keys: bfloat16 [32768, 64], P(('seq', 'head')), may hold values from -8 to 8
- key_weight: bfloat16 [512, 8192], P('seq', 'head'), may hold values from -0.25 to 0.25
- value_weight: bfloat16 [512, 8192], P('seq', 'head'), may hold values from -0.25 to 0.25
- doc_lengths: int32 [128], replicated, may hold values from 1 to 510, as said below
Outputs:
- attended: bfloat16 [32768, 8192], P(('seq', 'head'))
Inputs may be any that keep to these rules, and one draw needn't show every extreme that they name: `doc_lengths`: the documents lie in order in the pack and their lengths sum to 32768; document 0 starts at position 0 and every other document d starts strictly inside positions d * 256 to (d + 1) * 256 - 1, excluding the first of these; one length is exactly 510.
All inputs are finite; a program needn't handle non-finite values.
Results may differ from a plain program's by a relative error of at most 0.0062.
Values may be sent and summed in bfloat16 or wider, within the bound.
No kernel may reach another device: no remote copies, remote signals or barrier semaphores. Data moves between devices by JAX's collectives and lax.ppermute only.
A program may use at most 64 MiB of HBM per device.

v0:
```python
import functools
import math

import jax
import jax.numpy as jnp
from jax import lax
from jax.experimental import pallas as pl
from jax.experimental.pallas import tpu as pltpu
from jax.sharding import Mesh
from jax.sharding import PartitionSpec as P


NOPE = 128
ROPE = 64
VDIM = 128
WIDE = 256
SUB = 128
HALO = 512
SEQ = ("z", "y")
GROUP = ("x", "c")
EVERY = ("z", "y", "x", "c")
CHUNK = 512
STRIP = 16
VMEM_LIMIT = 24 * 2**20
INTERPRET = False
LOWEST = -1e30


def spread(value, axis):
    count = lax.axis_size(axis)
    copies = jnp.broadcast_to(value[None], (count, *value.shape))
    return lax.all_to_all(copies, axis, 0, 0)


def shifted(value, axes, steps):
    count = lax.axis_size(axes)
    return lax.ppermute(value, axes, [(i, i + steps) for i in range(count - steps)])


def turned(value, axis, steps):
    count = lax.axis_size(axis)
    return lax.ppermute(value, axis, [(i, (i + steps) % count) for i in range(count)])


def swapped(value):
    return lax.ppermute(value, "c", [(0, 1), (1, 0)])


def hops(step, flip):
    chips = lax.axis_size("x")
    return [
        (2 * x + c, 2 * ((x + step) % chips) + (c ^ flip)) for x in range(chips) for c in range(2)
    ]


def project_kernel(weight_rows, chips, at_ref, mine_ref, other_ref, *refs):
    weights, (k_ref, v_ref, w_ref, l_ref) = refs[:-4], refs[-4:]
    over_y = len(weights)
    for step, piece in enumerate(weights):
        at_y = lax.rem(at_ref[1] + over_y - step, over_y)
        for z in range(piece.shape[0] // weight_rows):
            at = pl.multiple_of((z * over_y + at_y) * weight_rows, weight_rows)
            w_ref[pl.ds(at, weight_rows), :] = piece[z * weight_rows : (z + 1) * weight_rows, :]
    rank = w_ref.shape[0]
    cols = v_ref.shape[1]
    for part, core in ((mine_ref, at_ref[2]), (other_ref, 1 - at_ref[2])):
        for i in range(part.shape[0] // SUB):
            chip = lax.rem(at_ref[0] + chips - i, chips) if i < chips else i - chips
            first = HALO if i < chips else 0
            at = pl.multiple_of(first + (2 * chip + core) * SUB, SUB)
            l_ref[pl.ds(at, SUB), :] = part[i * SUB : (i + 1) * SUB, :]

    for at in range(0, l_ref.shape[0], CHUNK):
        rows = slice(at, at + CHUNK)
        rope = l_ref[rows, rank:].astype(jnp.float32)
        rope_high = pltpu.roll(rope, ROPE, 1)
        low = lax.broadcasted_iota(jnp.int32, rope.shape, 1) < ROPE
        for col in range(0, 2 * cols, 256):
            product = jnp.dot(
                l_ref[rows, :rank], w_ref[:, col : col + 256], preferred_element_type=jnp.float32
            )
            if col >= cols:
                v_ref[rows, col - cols : col - cols + 256] = product.astype(jnp.bfloat16)
                continue
            moved = pltpu.roll(product[:, NOPE:], ROPE, 1)
            out = 2 * col
            k_ref[rows, out : out + 128] = product[:, :NOPE].astype(jnp.bfloat16)
            k_ref[rows, out + 128 : out + 256] = l_ref[rows, rank:]
            k_ref[rows, out + 256 : out + 384] = jnp.where(low, 0.0, moved).astype(jnp.bfloat16)
            k_ref[rows, out + 384 : out + 512] = jnp.where(low, moved, rope_high).astype(
                jnp.bfloat16
            )


IN_VMEM = pl.BlockSpec(memory_space=pltpu.VMEM)
IN_SMEM = pl.BlockSpec(memory_space=pltpu.SMEM)


def project(mine, other, weights):
    chips, over_y = lax.axis_size("x"), len(weights)
    rows = mine.shape[0] * 2
    cols = weights[0].shape[1] // 2
    rank = weights[0].shape[0] * over_y
    at = jnp.stack([lax.axis_index(axis) for axis in ("x", "y", "c")]).astype(jnp.int32)
    weight_rows = weights[0].shape[0] // lax.axis_size("z")
    return pl.pallas_call(
        functools.partial(project_kernel, weight_rows, chips),
        in_specs=[IN_SMEM] + [IN_VMEM] * (2 + over_y),
        out_specs=[IN_VMEM, IN_VMEM],
        scratch_shapes=[
            pltpu.VMEM((rank, 2 * cols), jnp.bfloat16),
            pltpu.VMEM((rows, mine.shape[1]), jnp.bfloat16),
        ],
        out_shape=[
            jax.ShapeDtypeStruct((rows, 2 * cols), jnp.bfloat16),
            jax.ShapeDtypeStruct((rows, cols), jnp.bfloat16),
        ],
        compiler_params=pltpu.CompilerParams(vmem_limit_bytes=VMEM_LIMIT),
        cost_estimate=pl.CostEstimate(
            flops=4 * rows * rank * cols, bytes_accessed=8 * rows * cols, transcendentals=0
        ),
        interpret=INTERPRET,
        name="project",
    )(at, mine, other, *weights)


def attend_kernel(
    score_scale, at_ref, q0_ref, q1_ref, k_ref, v_ref, start_ref, o0_ref, o1_ref, *scratch
):
    q_ref, o_ref, bias_ref, s_ref, p_ref, t_ref = scratch
    rows, window = 2 * SUB, 2 * SUB + HALO
    heads = v_ref.shape[1] // VDIM
    base = pl.multiple_of(at_ref[0], 2 * SUB)
    places = [pl.ds(pl.multiple_of(at_ref[1 + i], SUB), SUB) for i in range(2)]
    q_ref[places[0], :] = q0_ref[...]
    q_ref[places[1], :] = q1_ref[...]
    for at in range(0, rows, STRIP):
        row = lax.broadcasted_iota(jnp.int32, (STRIP, window), 0) + at
        col = lax.broadcasted_iota(jnp.int32, (STRIP, window), 1)
        start = start_ref[pl.ds(pl.multiple_of(base + at, STRIP), STRIP), :] - base
        allowed = (col <= row + HALO) & (col >= start)
        bias_ref[at : at + STRIP, :] = jnp.where(allowed, 0.0, LOWEST)
    span = pl.ds(base, window)

    @pl.loop(0, heads // 2)
    def _(pair):
        for half in range(2):
            q_at = pl.multiple_of(pair * 2 * (NOPE + ROPE) + 128 * half, 128)
            v_at = pl.ds(pl.multiple_of((2 * pair + half) * VDIM, VDIM), VDIM)
            k_at = pl.ds(pl.multiple_of((2 * pair + half) * WIDE, WIDE), WIDE)
            s_ref[half] = lax.dot_general(
                q_ref[:, pl.ds(q_at, WIDE)],
                k_ref[span, k_at],
                (((1,), (1,)), ((), ())),
                preferred_element_type=jnp.float32,
            )
        for half in range(2):
            v_at = pl.ds(pl.multiple_of((2 * pair + half) * VDIM, VDIM), VDIM)
            for at in range(0, rows, STRIP):
                part = slice(at, at + STRIP)
                scores = s_ref[half, part, :] * score_scale + bias_ref[part, :]
                expo = jnp.exp2(scores - jnp.max(scores, axis=1, keepdims=True))
                t_ref[half, part, :] = jnp.broadcast_to(
                    jnp.sum(expo, axis=1, keepdims=True), (STRIP, VDIM)
                )
                p_ref[half, part, :] = expo.astype(jnp.bfloat16)
            mixed = jnp.dot(p_ref[half], v_ref[span, v_at], preferred_element_type=jnp.float32)
            o_ref[:, v_at] = (mixed / t_ref[half]).astype(jnp.bfloat16)

    o0_ref[...] = o_ref[places[0], :]
    o1_ref[...] = o_ref[places[1], :]


def attend(chip, mine, other, keys, values, starts):
    rows, width = mine.shape
    heads = values.shape[1] // VDIM
    window = 2 * SUB + HALO
    core = lax.axis_index("c")
    at = jnp.stack([chip * 2 * SUB, core * SUB, (1 - core) * SUB]).astype(jnp.int32)
    score_scale = math.log2(math.e) / math.sqrt(NOPE + ROPE)
    o_shape = jax.ShapeDtypeStruct((rows, heads * VDIM), jnp.bfloat16)
    return pl.pallas_call(
        functools.partial(attend_kernel, score_scale),
        in_specs=[IN_SMEM] + [IN_VMEM] * 5,
        out_specs=[IN_VMEM, IN_VMEM],
        out_shape=[o_shape, o_shape],
        scratch_shapes=[
            pltpu.VMEM((2 * SUB, width), jnp.bfloat16),
            pltpu.VMEM((2 * SUB, heads * VDIM), jnp.bfloat16),
            pltpu.VMEM((2 * SUB, window), jnp.float32),
            pltpu.VMEM((2, 2 * SUB, window), jnp.float32),
            pltpu.VMEM((2, 2 * SUB, window), jnp.bfloat16),
            pltpu.VMEM((2, 2 * SUB, VDIM), jnp.float32),
        ],
        compiler_params=pltpu.CompilerParams(vmem_limit_bytes=VMEM_LIMIT),
        cost_estimate=pl.CostEstimate(
            flops=4 * heads * rows * window * (WIDE + VDIM),
            bytes_accessed=4 * rows * heads * 1024,
            transcendentals=2 * heads * rows * window,
        ),
        interpret=INTERPRET,
        name="attend",
    )(at, mine, other, keys, values, starts)


def whole(queries, latent, rope_keys, key_weight, value_weight, doc_lengths):
    tok_rows, _ = latent.shape
    chips = lax.axis_size("x")
    groups = 2 * chips
    group_rows = tok_rows * groups
    width = queries.shape[1] // groups
    x, core = lax.axis_index("x"), lax.axis_index("c")

    def block_of(step, flip):
        return 2 * lax.rem(x + step, chips) + (core ^ flip)

    weights = jnp.concatenate([key_weight, value_weight], axis=1)
    weights = spread(weights, "z").reshape(-1, weights.shape[1])
    over_y = lax.axis_size("y")
    weight_pieces = [weights] + [turned(weights, "y", s) for s in range(1, over_y)]

    both = jnp.concatenate(
        [latent, rope_keys, jnp.zeros((tok_rows, 128 - ROPE), jnp.bfloat16)], axis=1
    )
    parts = [both] + [turned(both, "x", s) for s in range(1, chips)]
    halo_chips = HALO // (2 * tok_rows)
    last = []
    for chip in range(chips - halo_chips, chips):
        behind = lax.rem(x + chips - chip, chips)
        last.append(lax.select_n(behind, *parts))
    last = jnp.concatenate(last, axis=0)
    earlier = shifted(last, SEQ, 1)
    mine = jnp.concatenate([*lax.optimization_barrier(parts), earlier], axis=0)
    other = swapped(mine)

    def sent(step, flip):
        out = lax.dynamic_slice_in_dim(queries, width * block_of(step, flip), width, 1)
        if not (step or flip):
            return out
        return lax.ppermute(out, GROUP, hops(step, flip))

    arrived = {(s, f): sent(s, f) for s in range(chips) for f in (0, 1)}

    docs = doc_lengths.shape[0]
    earlier = jnp.arange(docs)[None, :] < jnp.arange(docs)[:, None]
    starts = jnp.sum(jnp.where(earlier, doc_lengths[None, :], 0), axis=1)
    first_place = lax.axis_index(SEQ) * group_rows
    places = first_place + jnp.arange(group_rows, dtype=jnp.int32)
    own = jnp.max(
        jnp.where(starts[None, :] <= places[:, None], starts[None, :], 0), axis=1, keepdims=True
    )
    own = (own - first_place + HALO).astype(jnp.int32)

    keys, values = project(mine, other, weight_pieces)

    result = jnp.zeros((tok_rows, groups * value_weight.shape[1]), jnp.bfloat16)
    for step in (1, 3, 2, 0):
        chip = lax.rem(x + chips - step, chips)
        pair = attend(chip, arrived[step, 0], arrived[step, 1], keys, values, own)
        for flip in (0, 1):
            back = pair[flip]
            if step or flip:
                back = lax.ppermute(back, GROUP, [(b, a) for a, b in hops(step, flip)])
            at = value_weight.shape[1] * block_of(step, flip)
            result = lax.dynamic_update_slice(result, back, (0, at))
    return result


def solution(mesh):
    y = 4 if mesh.shape["seq"] % 4 == 0 else 1
    torus = Mesh(mesh.devices.reshape(-1, y, mesh.shape["head"] // 2, 2), EVERY)
    in_specs = (
        P(EVERY, None),
        P(EVERY, None),
        P(EVERY, None),
        P(SEQ, GROUP),
        P(SEQ, GROUP),
        P(),
    )
    return jax.shard_map(
        whole, mesh=torus, in_specs=in_specs, out_specs=P(EVERY, None), check_vma=False
    )
```

profile of v0, /device:TPU:33, one launch (start us, length us, event | category | flops | bytes accessed | tf_op | source)
XLA Modules:
  0.0 130.3 jit_solution(3068777415929458555)
XLA Ops:
  0.0 0.8 copy.13
  0.8 0.1 pad.15.clone
  0.9 0.9 maximum_maximum_fusion
  1.9 1.3 collective-permute-start.2
  3.1 2.5 %collective-permute-start.3 = (bf16[128,640]{1,0:T(8,128)(2,1)S(1)}, bf16[128,640]{1,0:T(8,128)(2,1)S(1)}, u32[]{:S(2)}, u32[]{:S(2)}) collective-permute-start(bf16[128,640]{1,0:T(8,128)(2,1)S(1)} %maximum_maximum_fusion), channel_id=1, source_target_pairs={{0,4},{2,6},{4,0},{6,2},{1,5},{3,7},{5,1},{7,3},{8,12},{10,14},{12... | collective-permute-start | bytes 491528 | tf_op jit(solution)/shard_map/ppermute | solution.py:42
  5.6 1.2 collective-permute-start.4
  6.8 0.8 pad_maximum_fusion.1
  7.5 0.8 broadcast_in_dim.43
  8.4 8.0 %all-to-all-start = ((bf16[8,16,2048]{2,1,0:T(8,128)(2,1)}), bf16[8,16,2048]{2,1,0:T(8,128)(2,1)S(1)}, u32[]{:S(2)}, u32[]{:S(2)}) async-start(bf16[8,16,2048]{2,1,0:T(8,128)(2,1)} %broadcast_in_dim.43), calls=%async_computation | async-start | bytes 1048576 | tf_op jit(solution)/shard_map/all_to_all | solution.py:32
  16.4 3.4 %constant_dynamic-slice_fusion = (bf16[128,1536]{1,0:T(8,128)(2,1)S(1)}, bf16[128,1536]{1,0:T(8,128)(2,1)}, bf16[128,1536]{1,0:T(8,128)(2,1)}, bf16[128,1536]{1,...) fusion(bf16[128,12288]{1,0:T(8,128)(2,1)} %param.6, ...), kind=kLoop, calls=%fused_computation.17 | loop fusion | bytes 6291488 | tf_op jit(solution)/shard_map/dynamic_slice | solution.py:237
  19.8 0.3 collective-permute-start
  20.1 0.1 select_reduce_fusion.1
  20.2 0.1 select_select_fusion.1
  20.4 3.2 %collective-permute-start.5 = (bf16[256,640]{1,0:T(8,128)(2,1)S(1)}, bf16[256,640]{1,0:T(8,128)(2,1)S(1)}, u32[]{:S(2)}, u32[]{:S(2)}) collective-permute-start(bf16[256,640]{1,0:T(8,128)(2,1)S(1)} %pad_maximum_fusion), channel_id=1, source_target_pairs={{0,8},{8,16},{16,24},{24,32},{32,40},{40,48},{48,56},{56,64},{64,7... | collective-permute-start | bytes 983048 | tf_op jit(solution)/shard_map/ppermute | solution.py:37
  23.7 13.1 %collective-permute-done.5 = bf16[256,640]{1,0:T(8,128)(2,1)S(1)} collective-permute-done((bf16[256,640]{1,0:T(8,128)(2,1)S(1)}, bf16[256,640]{1,0:T(8,128)(2,1)S(1)}, u32[]{:S(2)}, u32[]{:S(2)}) %collective-permute-start.5) | collective-permute-done | bytes 327712 | tf_op jit(solution)/shard_map/ppermute | solution.py:37
  36.9 2.2 %collective-permute-start.6 = (bf16[768,640]{1,0:T(8,128)(2,1)S(1)}, bf16[768,640]{1,0:T(8,128)(2,1)}, u32[]{:S(2)}, u32[]{:S(2)}) collective-permute-start(bf16[768,640]{1,0:T(8,128)(2,1)S(1)} %constant_dynamic-update-slice_fusion.mine_ref), channel_id=1, source_target_pairs={{0,1},{1,0},{2,3},{3,2},{4,5},{5,4},{6,7},{7,6},{8,9},{9,8},{10,11... | collective-permute-start | bytes 2949128 | tf_op jit(solution)/shard_map/ppermute | solution.py:46
  39.2 0.4 select_reduce_fusion
  39.6 0.2 copy.14.start_ref
  39.9 0.1 collective-permute-start.7
  40.0 0.4 collective-permute-start.8
  40.4 2.3 %collective-permute-start.9 = (bf16[128,2048]{1,0:T(8,128)(2,1)S(1)}, bf16[128,2048]{1,0:T(8,128)(2,1)S(1)}, u32[]{:S(2)}, u32[]{:S(2)}) collective-permute-start(bf16[128,2048]{1,0:T(8,128)(2,1)S(1)} %bitcast.13), channel_id=1, source_target_pairs={{0,24},{8,0},{16,8},{24,16},{1,25},{9,1},{17,9},{25,17},{2,26},{10... | collective-permute-start | bytes 1572872 | tf_op jit(solution)/shard_map/ppermute | solution.py:42
  42.7 0.8 collective-permute-start.1
  43.8 11.9 %collective-permute-done.1.q1_ref = bf16[128,1536]{1,0:T(8,128)(2,1)S(1)} collective-permute-done((bf16[128,1536]{1,0:T(8,128)(2,1)}, bf16[128,1536]{1,0:T(8,128)(2,1)S(1)}, u32[]{:S(2)}, u32[]{:S(2)}) %collective-permute-start.1) | collective-permute-done | bytes 393248 | tf_op jit(solution)/shard_map/ppermute | solution.py:240
  55.8 0.3 collective-permute-start.20
  56.1 9.8 %collective-permute-done.7.refs_1_ = bf16[128,2048]{1,0:T(8,128)(2,1)S(1)} collective-permute-done((bf16[128,2048]{1,0:T(8,128)(2,1)S(1)}, bf16[128,2048]{1,0:T(8,128)(2,1)S(1)}, u32[]{:S(2)}, u32[]{:S(2)}) %collective-permute-start.7) | collective-permute-done | bytes 524320 | tf_op jit(solution)/shard_map/ppermute | solution.py:42
  65.9 0.2 collective-permute-start.16
  66.1 3.8 %collective-permute-start.17 = (bf16[128,1536]{1,0:T(8,128)(2,1)}, bf16[128,1536]{1,0:T(8,128)(2,1)S(1)}, u32[]{:S(2)}, u32[]{:S(2)}) collective-permute-start(bf16[128,1536]{1,0:T(8,128)(2,1)} %get-tuple-element.34), channel_id=1, source_target_pairs={{0,5},{1,4},{2,7},{3,6},{4,1},{5,0},{6,3},{7,2},{8,13},{9,12},{10,... | collective-permute-start | bytes 1179656 | tf_op jit(solution)/shard_map/ppermute | solution.py:240
  69.9 0.6 collective-permute-start.13
  70.6 5.1 %project.1 = (bf16[1536,2048]{1,0:T(8,128)(2,1)S(1)}, bf16[1536,1024]{1,0:T(8,128)(2,1)S(1)}) custom-call(s32[3]{0:T(128)S(1)} %pad_add_fusion.at_ref, bf16[768,640]{1,0:T(8,128)(2,1)S(1)} %constant_dynamic-update-slice_fusion.mine_ref, bf16[768,640]{1,0:T(8,128)(2,1)} %collective-permute-done.6.other_ref, bf16[128,2048]{1,0:T(8,128)(2,1)S(1)} %bitcast.14, ...), custom_call_target="tpu_custom_call" | custom-call | flops 3221225472 | bytes 12582912 | tf_op jit(solution)/shard_map/project/pallas_call | solution.py:106
  75.7 4.3 %attend.4 = (bf16[128,1024]{1,0:T(8,128)(2,1)S(1)}, bf16[128,1024]{1,0:T(8,128)(2,1)S(1)}) custom-call(s32[3]{0:T(128)S(1)} %add_add_fusion.at_ref, bf16[128,1536]{1,0:T(8,128)(2,1)S(1)} %collective-permute-done.q0_ref, bf16[128,1536]{1,0:T(8,128)(2,1)S(1)} %collective-permute-done.1.q1_ref, bf16[1536,2048]{1,0:T(8,128)(2,1)S(1)} %get-tuple-element.23.k_ref, ...), custom_call_target="tpu_custom_call" | custom-call | flops 1207959552 | bytes 4194304 | tf_op jit(solution)/shard_map/attend/pallas_call | solution.py:182
  80.0 1.3 %collective-permute-start.10 = (bf16[128,1024]{1,0:T(8,128)(2,1)S(1)}, bf16[128,1024]{1,0:T(8,128)(2,1)S(1)}, u32[]{:S(2)}, u32[]{:S(2)}) collective-permute-start(bf16[128,1024]{1,0:T(8,128)(2,1)S(1)} %get-tuple-element.25), channel_id=1, source_target_pairs={{2,0},{3,1},{4,2},{5,3},{6,4},{7,5},{0,6},{1,7},{10,8},{11,9},{12,... | collective-permute-start | bytes 786440 | tf_op jit(solution)/shard_map/ppermute | solution.py:263
  81.4 5.5 %collective-permute-done.17.q1_ref = bf16[128,1536]{1,0:T(8,128)(2,1)S(1)} collective-permute-done((bf16[128,1536]{1,0:T(8,128)(2,1)}, bf16[128,1536]{1,0:T(8,128)(2,1)S(1)}, u32[]{:S(2)}, u32[]{:S(2)}) %collective-permute-start.17) | collective-permute-done | bytes 393248 | tf_op jit(solution)/shard_map/ppermute | solution.py:240
  86.9 4.3 %attend.6 = (bf16[128,1024]{1,0:T(8,128)(2,1)S(1)}, bf16[128,1024]{1,0:T(8,128)(2,1)S(1)}) custom-call(s32[3]{0:T(128)S(1)} %add_add_fusion.2.at_ref, bf16[128,1536]{1,0:T(8,128)(2,1)S(1)} %collective-permute-done.16.q0_ref, bf16[128,1536]{1,0:T(8,128)(2,1)S(1)} %collective-permute-done.17.q1_ref, bf16[1536,2048]{1,0:T(8,128)(2,1)S(1)} %get-tuple-element.23.k_ref, ...), custom_call_target="tpu_custom_call" | custom-call | flops 1207959552 | bytes 4194304 | tf_op jit(solution)/shard_map/attend/pallas_call | solution.py:182
  91.2 0.3 collective-permute-start.18
  91.5 0.7 collective-permute-done.12.q0_ref
  92.2 4.2 %collective-permute-start.11 = (bf16[128,1024]{1,0:T(8,128)(2,1)S(1)}, bf16[128,1024]{1,0:T(8,128)(2,1)S(1)}, u32[]{:S(2)}, u32[]{:S(2)}) collective-permute-start(bf16[128,1024]{1,0:T(8,128)(2,1)S(1)} %get-tuple-element.26), channel_id=1, source_target_pairs={{3,0},{2,1},{5,2},{4,3},{7,4},{6,5},{1,6},{0,7},{11,8},{10,9},{13,... | collective-permute-start | bytes 786440 | tf_op jit(solution)/shard_map/ppermute | solution.py:263
  96.3 6.3 %collective-permute-done.13.q1_ref = bf16[128,1536]{1,0:T(8,128)(2,1)S(1)} collective-permute-done((bf16[128,1536]{1,0:T(8,128)(2,1)}, bf16[128,1536]{1,0:T(8,128)(2,1)S(1)}, u32[]{:S(2)}, u32[]{:S(2)}) %collective-permute-start.13) | collective-permute-done | bytes 393248 | tf_op jit(solution)/shard_map/ppermute | solution.py:240
  102.7 4.3 %attend.5 = (bf16[128,1024]{1,0:T(8,128)(2,1)S(1)}, bf16[128,1024]{1,0:T(8,128)(2,1)S(1)}) custom-call(s32[3]{0:T(128)S(1)} %add_add_fusion.1.at_ref, bf16[128,1536]{1,0:T(8,128)(2,1)S(1)} %collective-permute-done.12.q0_ref, bf16[128,1536]{1,0:T(8,128)(2,1)S(1)} %collective-permute-done.13.q1_ref, bf16[1536,2048]{1,0:T(8,128)(2,1)S(1)} %get-tuple-element.23.k_ref, ...), custom_call_target="tpu_custom_call" | custom-call | flops 1207959552 | bytes 4194304 | tf_op jit(solution)/shard_map/attend/pallas_call | solution.py:182
  107.0 1.7 %collective-permute-start.14 = (bf16[128,1024]{1,0:T(8,128)(2,1)S(1)}, bf16[128,1024]{1,0:T(8,128)(2,1)S(1)}, u32[]{:S(2)}, u32[]{:S(2)}) collective-permute-start(bf16[128,1024]{1,0:T(8,128)(2,1)S(1)} %get-tuple-element.27), channel_id=1, source_target_pairs={{6,0},{7,1},{0,2},{1,3},{2,4},{3,5},{4,6},{5,7},{14,8},{15,9},{8,1... | collective-permute-start | bytes 786440 | tf_op jit(solution)/shard_map/ppermute | solution.py:263
  108.7 0.4 collective-permute-start.15
  109.1 4.3 %attend.7 = (bf16[128,1024]{1,0:T(8,128)(2,1)S(1)}, bf16[128,1024]{1,0:T(8,128)(2,1)S(1)}) custom-call(s32[3]{0:T(128)S(1)} %add_add_fusion.3.at_ref, bf16[128,1536]{1,0:T(8,128)(2,1)S(1)} %get-tuple-element.40.q0_ref, bf16[128,1536]{1,0:T(8,128)(2,1)S(1)} %collective-permute-done.20.q1_ref, bf16[1536,2048]{1,0:T(8,128)(2,1)S(1)} %get-tuple-element.23.k_ref, ...), custom_call_target="tpu_custom_call" | custom-call | flops 1207959552 | bytes 4194304 | tf_op jit(solution)/shard_map/attend/pallas_call | solution.py:182
  113.4 2.2 %collective-permute-start.19 = (bf16[128,1024]{1,0:T(8,128)(2,1)S(1)}, bf16[128,1024]{1,0:T(8,128)(2,1)S(1)}, u32[]{:S(2)}, u32[]{:S(2)}) collective-permute-start(bf16[128,1024]{1,0:T(8,128)(2,1)S(1)} %get-tuple-element.30), channel_id=1, source_target_pairs={{5,0},{4,1},{7,2},{6,3},{1,4},{0,5},{3,6},{2,7},{13,8},{12,9},{15,... | collective-permute-start | bytes 786440 | tf_op jit(solution)/shard_map/ppermute | solution.py:263
  115.6 0.2 broadcast_in_dim.28
  115.9 3.3 %collective-permute-done.11 = bf16[128,1024]{1,0:T(8,128)(2,1)S(1)} collective-permute-done((bf16[128,1024]{1,0:T(8,128)(2,1)S(1)}, bf16[128,1024]{1,0:T(8,128)(2,1)S(1)}, u32[]{:S(2)}, u32[]{:S(2)}) %collective-permute-start.11) | collective-permute-done | bytes 262176 | tf_op jit(solution)/shard_map/ppermute | solution.py:263
  119.2 2.5 %collective-permute-done.15 = bf16[128,1024]{1,0:T(8,128)(2,1)S(1)} collective-permute-done((bf16[128,1024]{1,0:T(8,128)(2,1)S(1)}, bf16[128,1024]{1,0:T(8,128)(2,1)S(1)}, u32[]{:S(2)}, u32[]{:S(2)}) %collective-permute-start.15) | collective-permute-done | bytes 262176 | tf_op jit(solution)/shard_map/ppermute | solution.py:263
  121.8 6.5 %collective-permute-done.19 = bf16[128,1024]{1,0:T(8,128)(2,1)S(1)} collective-permute-done((bf16[128,1024]{1,0:T(8,128)(2,1)S(1)}, bf16[128,1024]{1,0:T(8,128)(2,1)S(1)}, u32[]{:S(2)}, u32[]{:S(2)}) %collective-permute-start.19) | collective-permute-done | bytes 262176 | tf_op jit(solution)/shard_map/ppermute | solution.py:263
  128.3 1.3 copy-done
  129.6 0.7 constant_dynamic-update-slice_fusion.5
  (42 shorter events, 0.8 us)
Async XLA Ops:
  1.9 18.3 %collective-permute-start.2 = (bf16[128,640]{1,0:T(8,128)(2,1)S(1)}, bf16[128,640]{1,0:T(8,128)(2,1)S(1)}, u32[]{:S(2)}, u32[]{:S(2)}) collective-permute-start(bf16[128,640]{1,0:T(8,128)(2,1)S(1)} %maximum_maximum_fusion), channel_id=1, source_target_pairs={{0,2},{2,4},{4,6},{6,0},{1,3},{3,5},{5,7},{7,1},{8,10},{10,12},{12... | collective-permute-start | bytes 491528 | tf_op jit(solution)/shard_map/ppermute | solution.py:42
  3.1 17.0 %collective-permute-start.3 = (bf16[128,640]{1,0:T(8,128)(2,1)S(1)}, bf16[128,640]{1,0:T(8,128)(2,1)S(1)}, u32[]{:S(2)}, u32[]{:S(2)}) collective-permute-start(bf16[128,640]{1,0:T(8,128)(2,1)S(1)} %maximum_maximum_fusion), channel_id=1, source_target_pairs={{0,4},{2,6},{4,0},{6,2},{1,5},{3,7},{5,1},{7,3},{8,12},{10,14},{12... | collective-permute-start | bytes 491528 | tf_op jit(solution)/shard_map/ppermute | solution.py:42
  5.6 14.6 %collective-permute-start.4 = (bf16[128,640]{1,0:T(8,128)(2,1)S(1)}, bf16[128,640]{1,0:T(8,128)(2,1)S(1)}, u32[]{:S(2)}, u32[]{:S(2)}) collective-permute-start(bf16[128,640]{1,0:T(8,128)(2,1)S(1)} %maximum_maximum_fusion), channel_id=1, source_target_pairs={{0,6},{2,0},{4,2},{6,4},{1,7},{3,1},{5,3},{7,5},{8,14},{10,8},{12,... | collective-permute-start | bytes 491528 | tf_op jit(solution)/shard_map/ppermute | solution.py:42
  8.4 31.5 %all-to-all-start = ((bf16[8,16,2048]{2,1,0:T(8,128)(2,1)}), bf16[8,16,2048]{2,1,0:T(8,128)(2,1)S(1)}, u32[]{:S(2)}, u32[]{:S(2)}) async-start(bf16[8,16,2048]{2,1,0:T(8,128)(2,1)} %broadcast_in_dim.43), calls=%async_computation | async-start | bytes 1048576 | tf_op jit(solution)/shard_map/all_to_all | solution.py:32
  16.4 3.7 %copy-start.2 = (s32[128]{0:T(128)S(1)}, s32[128]{0:T(128)}, u32[]{:S(2)}) copy-start(s32[128]{0:T(128)} %param.11) | copy-start | bytes 1540
  16.4 3.8 %copy-start.1 = (bf16[128,512]{1,0:T(8,128)(2,1)S(1)}, bf16[128,512]{1,0:T(8,128)(2,1)}, u32[]{:S(2)}) copy-start(bf16[128,512]{1,0:T(8,128)(2,1)} %param.7) | copy-start | bytes 393220
  19.8 23.0 %collective-permute-start = (bf16[128,1536]{1,0:T(8,128)(2,1)}, bf16[128,1536]{1,0:T(8,128)(2,1)S(1)}, u32[]{:S(2)}, u32[]{:S(2)}) collective-permute-start(bf16[128,1536]{1,0:T(8,128)(2,1)} %get-tuple-element.39), channel_id=1, source_target_pairs={{0,2},{1,3},{2,4},{3,5},{4,6},{5,7},{6,0},{7,1},{8,10},{9,11},{10,... | collective-permute-start | bytes 1179656 | tf_op jit(solution)/shard_map/ppermute | solution.py:240
  20.4 16.5 %collective-permute-start.5 = (bf16[256,640]{1,0:T(8,128)(2,1)S(1)}, bf16[256,640]{1,0:T(8,128)(2,1)S(1)}, u32[]{:S(2)}, u32[]{:S(2)}) collective-permute-start(bf16[256,640]{1,0:T(8,128)(2,1)S(1)} %pad_maximum_fusion), channel_id=1, source_target_pairs={{0,8},{8,16},{16,24},{24,32},{32,40},{40,48},{48,56},{56,64},{64,7... | collective-permute-start | bytes 983048 | tf_op jit(solution)/shard_map/ppermute | solution.py:37
  36.9 33.0 %collective-permute-start.6 = (bf16[768,640]{1,0:T(8,128)(2,1)S(1)}, bf16[768,640]{1,0:T(8,128)(2,1)}, u32[]{:S(2)}, u32[]{:S(2)}) collective-permute-start(bf16[768,640]{1,0:T(8,128)(2,1)S(1)} %constant_dynamic-update-slice_fusion.mine_ref), channel_id=1, source_target_pairs={{0,1},{1,0},{2,3},{3,2},{4,5},{5,4},{6,7},{7,6},{8,9},{9,8},{10,11... | collective-permute-start | bytes 2949128 | tf_op jit(solution)/shard_map/ppermute | solution.py:46
  39.9 26.0 %collective-permute-start.7 = (bf16[128,2048]{1,0:T(8,128)(2,1)S(1)}, bf16[128,2048]{1,0:T(8,128)(2,1)S(1)}, u32[]{:S(2)}, u32[]{:S(2)}) collective-permute-start(bf16[128,2048]{1,0:T(8,128)(2,1)S(1)} %bitcast.11), channel_id=1, source_target_pairs={{0,8},{8,16},{16,24},{24,0},{1,9},{9,17},{17,25},{25,1},{2,10},{10... | collective-permute-start | bytes 1572872 | tf_op jit(solution)/shard_map/ppermute | solution.py:42
  40.0 26.1 %collective-permute-start.8 = (bf16[128,2048]{1,0:T(8,128)(2,1)S(1)}, bf16[128,2048]{1,0:T(8,128)(2,1)S(1)}, u32[]{:S(2)}, u32[]{:S(2)}) collective-permute-start(bf16[128,2048]{1,0:T(8,128)(2,1)S(1)} %bitcast.12), channel_id=1, source_target_pairs={{0,16},{8,24},{16,0},{24,8},{1,17},{9,25},{17,1},{25,9},{2,18},{10... | collective-permute-start | bytes 1572872 | tf_op jit(solution)/shard_map/ppermute | solution.py:42
  40.4 29.5 %collective-permute-start.9 = (bf16[128,2048]{1,0:T(8,128)(2,1)S(1)}, bf16[128,2048]{1,0:T(8,128)(2,1)S(1)}, u32[]{:S(2)}, u32[]{:S(2)}) collective-permute-start(bf16[128,2048]{1,0:T(8,128)(2,1)S(1)} %bitcast.13), channel_id=1, source_target_pairs={{0,24},{8,0},{16,8},{24,16},{1,25},{9,1},{17,9},{25,17},{2,26},{10... | collective-permute-start | bytes 1572872 | tf_op jit(solution)/shard_map/ppermute | solution.py:42
  42.7 13.0 %collective-permute-start.1 = (bf16[128,1536]{1,0:T(8,128)(2,1)}, bf16[128,1536]{1,0:T(8,128)(2,1)S(1)}, u32[]{:S(2)}, u32[]{:S(2)}) collective-permute-start(bf16[128,1536]{1,0:T(8,128)(2,1)} %get-tuple-element.38), channel_id=1, source_target_pairs={{0,3},{1,2},{2,5},{3,4},{4,7},{5,6},{6,1},{7,0},{8,11},{9,10},{10,... | collective-permute-start | bytes 1179656 | tf_op jit(solution)/shard_map/ppermute | solution.py:240
  55.8 52.9 %collective-permute-start.20 = (bf16[128,1536]{1,0:T(8,128)(2,1)S(1)}, bf16[128,1536]{1,0:T(8,128)(2,1)S(1)}, u32[]{:S(2)}, u32[]{:S(2)}) collective-permute-start(bf16[128,1536]{1,0:T(8,128)(2,1)S(1)} %get-tuple-element.33), channel_id=1, source_target_pairs={{0,1},{1,0},{2,3},{3,2},{4,5},{5,4},{6,7},{7,6},{8,9},{9,8},{10,11... | collective-permute-start | bytes 1179656 | tf_op jit(solution)/shard_map/ppermute | solution.py:240
  65.9 14.1 %collective-permute-start.16 = (bf16[128,1536]{1,0:T(8,128)(2,1)}, bf16[128,1536]{1,0:T(8,128)(2,1)S(1)}, u32[]{:S(2)}, u32[]{:S(2)}) collective-permute-start(bf16[128,1536]{1,0:T(8,128)(2,1)} %get-tuple-element.35), channel_id=1, source_target_pairs={{0,4},{1,5},{2,6},{3,7},{4,0},{5,1},{6,2},{7,3},{8,12},{9,13},{10,... | collective-permute-start | bytes 1179656 | tf_op jit(solution)/shard_map/ppermute | solution.py:240
  66.1 20.8 %collective-permute-start.17 = (bf16[128,1536]{1,0:T(8,128)(2,1)}, bf16[128,1536]{1,0:T(8,128)(2,1)S(1)}, u32[]{:S(2)}, u32[]{:S(2)}) collective-permute-start(bf16[128,1536]{1,0:T(8,128)(2,1)} %get-tuple-element.34), channel_id=1, source_target_pairs={{0,5},{1,4},{2,7},{3,6},{4,1},{5,0},{6,3},{7,2},{8,13},{9,12},{10,... | collective-permute-start | bytes 1179656 | tf_op jit(solution)/shard_map/ppermute | solution.py:240
  69.9 22.3 %collective-permute-start.12 = (bf16[128,1536]{1,0:T(8,128)(2,1)}, bf16[128,1536]{1,0:T(8,128)(2,1)S(1)}, u32[]{:S(2)}, u32[]{:S(2)}) collective-permute-start(bf16[128,1536]{1,0:T(8,128)(2,1)} %get-tuple-element.37), channel_id=1, source_target_pairs={{0,6},{1,7},{2,0},{3,1},{4,2},{5,3},{6,4},{7,5},{8,14},{9,15},{10,... | collective-permute-start | bytes 1179656 | tf_op jit(solution)/shard_map/ppermute | solution.py:240
  69.9 32.7 %collective-permute-start.13 = (bf16[128,1536]{1,0:T(8,128)(2,1)}, bf16[128,1536]{1,0:T(8,128)(2,1)S(1)}, u32[]{:S(2)}, u32[]{:S(2)}) collective-permute-start(bf16[128,1536]{1,0:T(8,128)(2,1)} %get-tuple-element.36), channel_id=1, source_target_pairs={{0,7},{1,6},{2,1},{3,0},{4,3},{5,2},{6,5},{7,4},{8,15},{9,14},{10,... | collective-permute-start | bytes 1179656 | tf_op jit(solution)/shard_map/ppermute | solution.py:240
  80.0 33.4 %collective-permute-start.10 = (bf16[128,1024]{1,0:T(8,128)(2,1)S(1)}, bf16[128,1024]{1,0:T(8,128)(2,1)S(1)}, u32[]{:S(2)}, u32[]{:S(2)}) collective-permute-start(bf16[128,1024]{1,0:T(8,128)(2,1)S(1)} %get-tuple-element.25), channel_id=1, source_target_pairs={{2,0},{3,1},{4,2},{5,3},{6,4},{7,5},{0,6},{1,7},{10,8},{11,9},{12,... | collective-permute-start | bytes 786440 | tf_op jit(solution)/shard_map/ppermute | solution.py:263
  91.2 30.5 %collective-permute-start.18 = (bf16[128,1024]{1,0:T(8,128)(2,1)S(1)}, bf16[128,1024]{1,0:T(8,128)(2,1)S(1)}, u32[]{:S(2)}, u32[]{:S(2)}) collective-permute-start(bf16[128,1024]{1,0:T(8,128)(2,1)S(1)} %get-tuple-element.29), channel_id=1, source_target_pairs={{4,0},{5,1},{6,2},{7,3},{0,4},{1,5},{2,6},{3,7},{12,8},{13,9},{14,... | collective-permute-start | bytes 786440 | tf_op jit(solution)/shard_map/ppermute | solution.py:263
  92.2 26.9 %collective-permute-start.11 = (bf16[128,1024]{1,0:T(8,128)(2,1)S(1)}, bf16[128,1024]{1,0:T(8,128)(2,1)S(1)}, u32[]{:S(2)}, u32[]{:S(2)}) collective-permute-start(bf16[128,1024]{1,0:T(8,128)(2,1)S(1)} %get-tuple-element.26), channel_id=1, source_target_pairs={{3,0},{2,1},{5,2},{4,3},{7,4},{6,5},{1,6},{0,7},{11,8},{10,9},{13,... | collective-permute-start | bytes 786440 | tf_op jit(solution)/shard_map/ppermute | solution.py:263
  107.0 12.2 %collective-permute-start.14 = (bf16[128,1024]{1,0:T(8,128)(2,1)S(1)}, bf16[128,1024]{1,0:T(8,128)(2,1)S(1)}, u32[]{:S(2)}, u32[]{:S(2)}) collective-permute-start(bf16[128,1024]{1,0:T(8,128)(2,1)S(1)} %get-tuple-element.27), channel_id=1, source_target_pairs={{6,0},{7,1},{0,2},{1,3},{2,4},{3,5},{4,6},{5,7},{14,8},{15,9},{8,1... | collective-permute-start | bytes 786440 | tf_op jit(solution)/shard_map/ppermute | solution.py:263
  108.7 13.0 %collective-permute-start.15 = (bf16[128,1024]{1,0:T(8,128)(2,1)S(1)}, bf16[128,1024]{1,0:T(8,128)(2,1)S(1)}, u32[]{:S(2)}, u32[]{:S(2)}) collective-permute-start(bf16[128,1024]{1,0:T(8,128)(2,1)S(1)} %get-tuple-element.28), channel_id=1, source_target_pairs={{7,0},{6,1},{1,2},{0,3},{3,4},{2,5},{5,6},{4,7},{15,8},{14,9},{9,1... | collective-permute-start | bytes 786440 | tf_op jit(solution)/shard_map/ppermute | solution.py:263
  113.4 14.8 %collective-permute-start.19 = (bf16[128,1024]{1,0:T(8,128)(2,1)S(1)}, bf16[128,1024]{1,0:T(8,128)(2,1)S(1)}, u32[]{:S(2)}, u32[]{:S(2)}) collective-permute-start(bf16[128,1024]{1,0:T(8,128)(2,1)S(1)} %get-tuple-element.30), channel_id=1, source_target_pairs={{5,0},{4,1},{7,2},{6,3},{1,4},{0,5},{3,6},{2,7},{13,8},{12,9},{15,... | collective-permute-start | bytes 786440 | tf_op jit(solution)/shard_map/ppermute | solution.py:263
  119.1 9.2 %collective-permute-start.21 = (bf16[128,1024]{1,0:T(8,128)(2,1)S(1)}, bf16[128,1024]{1,0:T(8,128)(2,1)S(1)}, u32[]{:S(2)}, u32[]{:S(2)}) collective-permute-start(bf16[128,1024]{1,0:T(8,128)(2,1)S(1)} %get-tuple-element.32), channel_id=1, source_target_pairs={{1,0},{0,1},{3,2},{2,3},{5,4},{4,5},{7,6},{6,7},{9,8},{8,9},{11,10... | collective-permute-start | bytes 786440 | tf_op jit(solution)/shard_map/ppermute | solution.py:263
  128.3 1.3 %copy-start = (bf16[128,8192]{1,0:T(8,128)(2,1)}, bf16[128,8192]{1,0:T(8,128)(2,1)S(1)}, u32[]{:S(2)}) copy-start(bf16[128,8192]{1,0:T(8,128)(2,1)S(1)} %constant_dynamic-update-slice_fusion.6) | copy-start | bytes 6291460
where the time goes:
time: 131 us; the launch traced here: 130 us
  waiting for transfers between devices  59.6 us (45%)
  starting transfers between devices  37.3 us (28%)
  Pallas kernels  22.4 us (17%)
  local copies, waits for them, and re-layouts  7.84 us (6%)
  other arithmetic  2.75 us (2%)
    ppermute x7, waiting for transfers between devices, sent(): return lax.ppermute(out, GROUP, hops(step, flip))  24.5 us
    pallas_call x4, Pallas kernels, attend(): pl.pallas_call(functools.partial(attend_kernel, score_scale), in_specs=[I...  17.3 us
    ppermute x1, waiting for transfers between devices, shifted(): lax.ppermute(value, axes, [(i, i + steps) for i in range(count - steps)])  13.1 us
    ppermute x7, waiting for transfers between devices, whole(): back = lax.ppermute(back, GROUP, [(b, a) for a, b in hops(step, flip)])  12.2 us
    ppermute x7, starting transfers between devices, whole(): back = lax.ppermute(back, GROUP, [(b, a) for a, b in hops(step, flip)])  10.1 us
    ppermute x6, waiting for transfers between devices, turned(): lax.ppermute(value, axis, [(i, (i + steps) % count) for i in range(count)])  9.82 us
    all_to_all x1, starting transfers between devices, spread(): return lax.all_to_all(copies, axis, 0, 0)  8.01 us
    ppermute x6, starting transfers between devices, turned(): lax.ppermute(value, axis, [(i, (i + steps) % count) for i in range(count)])  7.64 us
  transfers between devices with their start and end apart: 23, of which 9 were waited for; matrix products, arithmetic and copies ran while one was open for 5% of the time, Pallas kernels for 17%

commit v1 on v0

--- a/solution.py
+++ b/solution.py
@@ -53,14 +53,18 @@
     ]
 
 
-def project_kernel(weight_rows, chips, at_ref, mine_ref, other_ref, *refs):
-    weights, (k_ref, v_ref, w_ref, l_ref) = refs[:-4], refs[-4:]
-    over_y = len(weights)
-    for step, piece in enumerate(weights):
+def project_kernel(weight_rows, places, chips, at_ref, mine_ref, other_ref, *refs):
+    weights, (k_ref, v_ref, w_ref, l_ref) = iter(refs[:-4]), refs[-4:]
+    over_y = len(places)
+    for step, parts in places:
         at_y = lax.rem(at_ref[1] + over_y - step, over_y)
-        for z in range(piece.shape[0] // weight_rows):
-            at = pl.multiple_of((z * over_y + at_y) * weight_rows, weight_rows)
-            w_ref[pl.ds(at, weight_rows), :] = piece[z * weight_rows : (z + 1) * weight_rows, :]
+        z = 0
+        for _ in range(parts):
+            piece = next(weights)
+            for row in range(0, piece.shape[0], weight_rows):
+                at = pl.multiple_of((z * over_y + at_y) * weight_rows, weight_rows)
+                w_ref[pl.ds(at, weight_rows), :] = piece[row : row + weight_rows, :]
+                z += 1
     rank = w_ref.shape[0]
     cols = v_ref.shape[1]
     for part, core in ((mine_ref, at_ref[2]), (other_ref, 1 - at_ref[2])):
@@ -96,16 +100,42 @@
 IN_SMEM = pl.BlockSpec(memory_space=pltpu.SMEM)
 
 
+def joined_kernel(*refs):
+    *parts, out_ref = refs
+    at = 0
+    for part in parts:
+        out_ref[at : at + part.shape[0], :] = part[...]
+        at += part.shape[0]
+
+
+def joined(parts):
+    rows = sum(part.shape[0] for part in parts)
+    return pl.pallas_call(
+        joined_kernel,
+        in_specs=[IN_VMEM] * len(parts),
+        out_specs=IN_VMEM,
+        out_shape=jax.ShapeDtypeStruct((rows, parts[0].shape[1]), parts[0].dtype),
+        compiler_params=pltpu.CompilerParams(vmem_limit_bytes=VMEM_LIMIT),
+        cost_estimate=pl.CostEstimate(
+            flops=rows * 1024, bytes_accessed=rows * 2560, transcendentals=0
+        ),
+        interpret=INTERPRET,
+        name="joined",
+    )(*parts)
+
+
 def project(mine, other, weights):
-    chips, over_y = lax.axis_size("x"), len(weights)
+    chips = lax.axis_size("x")
     rows = mine.shape[0] * 2
+    places = tuple((step, len(parts)) for step, *parts in weights)
+    weights = [part for _, *parts in weights for part in parts]
     cols = weights[0].shape[1] // 2
-    rank = weights[0].shape[0] * over_y
+    rank = weights[0].shape[0] * len(places)
     at = jnp.stack([lax.axis_index(axis) for axis in ("x", "y", "c")]).astype(jnp.int32)
     weight_rows = weights[0].shape[0] // lax.axis_size("z")
     return pl.pallas_call(
-        functools.partial(project_kernel, weight_rows, chips),
-        in_specs=[IN_SMEM] + [IN_VMEM] * (2 + over_y),
+        functools.partial(project_kernel, weight_rows, places, chips),
+        in_specs=[IN_SMEM] + [IN_VMEM] * (2 + len(weights)),
         out_specs=[IN_VMEM, IN_VMEM],
         scratch_shapes=[
             pltpu.VMEM((rank, 2 * cols), jnp.bfloat16),
@@ -217,7 +247,7 @@
     weights = jnp.concatenate([key_weight, value_weight], axis=1)
     weights = spread(weights, "z").reshape(-1, weights.shape[1])
     over_y = lax.axis_size("y")
-    weight_pieces = [weights] + [turned(weights, "y", s) for s in range(1, over_y)]
+    weight_pieces = [(s, turned(weights, "y", s) if s else weights) for s in range(over_y)]
 
     both = jnp.concatenate(
         [latent, rope_keys, jnp.zeros((tok_rows, 128 - ROPE), jnp.bfloat16)], axis=1
@@ -230,11 +260,13 @@
         last.append(lax.select_n(behind, *parts))
     last = jnp.concatenate(last, axis=0)
     earlier = shifted(last, SEQ, 1)
-    mine = jnp.concatenate([*lax.optimization_barrier(parts), earlier], axis=0)
+    mine = joined([*parts, earlier])
     other = swapped(mine)
 
+    late, _ = lax.optimization_barrier((queries, last))
+
     def sent(step, flip):
-        out = lax.dynamic_slice_in_dim(queries, width * block_of(step, flip), width, 1)
+        out = lax.dynamic_slice_in_dim(queries if step % 2 else late, width * block_of(step, flip), width, 1)
         if not (step or flip):
             return out
         return lax.ppermute(out, GROUP, hops(step, flip))
@@ -254,7 +286,7 @@
     keys, values = project(mine, other, weight_pieces)
 
     result = jnp.zeros((tok_rows, groups * value_weight.shape[1]), jnp.bfloat16)
-    for step in (1, 3, 2, 0):
+    for step in (2, 1, 3, 0):
         chip = lax.rem(x + chips - step, chips)
         pair = attend(chip, arrived[step, 0], arrived[step, 1], keys, values, own)
         for flip in (0, 1):

time: 131 us -> 117 us (0.89)
  waiting for transfers between devices: 59.6 us -> 47.5 us
    ppermute x6, waiting for transfers between devices: 9.82 us -> 0.26 us  [turned(): lax.ppermute(value, axis, [(i, (i + steps) % count) for i in range(count)])]
    ppermute x7, waiting for transfers between devices: 12.2 us -> 7 us  [whole(): back = lax.ppermute(back, GROUP, [(b, a) for a, b in hops(step, flip)])]
    ppermute x1, waiting for transfers between devices: 13.1 us -> 16.1 us  [shifted(): lax.ppermute(value, axes, [(i, i + steps) for i in range(count - steps)])]
    dynamic_slice x1 -> x2, local copies, waits for them, and re-layouts: 3.36 us -> 2.5 us  [sent(): lax.dynamic_slice_in_dim(queries if step % 2 else late, width * block_of(...]
    pallas_call x1 -> x2, Pallas kernels: 5.13 us -> 5.65 us  [the longest x1 5.57 us: project(): pl.pallas_call(functools.partial(project_kernel, weight_rows, places, chi...]
  transfers between devices with their start and end apart: 23 -> 23, of which waited for: 9 -> 8; matrix products, arithmetic and copies ran while one was open for 5% -> 5% of each run, Pallas kernels for 17% -> 20%
where the time goes in v1:
time: 117 us
  waiting for transfers between devices  47.5 us (41%)
  starting transfers between devices  36.4 us (31%)
  Pallas kernels  22.9 us (20%)
  local copies, waits for them, and re-layouts  6.89 us (6%)
  other arithmetic  2.76 us (2%)
    ppermute x7, waiting for transfers between devices, sent(): return lax.ppermute(out, GROUP, hops(step, flip))  24.1 us
    pallas_call x4, Pallas kernels, attend(): pl.pallas_call(functools.partial(attend_kernel, score_scale), in_specs=[I...  17.3 us
    ppermute x1, waiting for transfers between devices, shifted(): lax.ppermute(value, axes, [(i, i + steps) for i in range(count - steps)])  16.1 us
    ppermute x7, starting transfers between devices, whole(): back = lax.ppermute(back, GROUP, [(b, a) for a, b in hops(step, flip)])  9.35 us
    all_to_all x1, starting transfers between devices, spread(): return lax.all_to_all(copies, axis, 0, 0)  8.01 us
    ppermute x6, starting transfers between devices, turned(): lax.ppermute(value, axis, [(i, (i + steps) % count) for i in range(count)])  7.62 us
    ppermute x7, waiting for transfers between devices, whole(): back = lax.ppermute(back, GROUP, [(b, a) for a, b in hops(step, flip)])  7 us
    ppermute x7, starting transfers between devices, sent(): return lax.ppermute(out, GROUP, hops(step, flip))  5.63 us
  transfers between devices with their start and end apart: 23, of which 8 were waited for; matrix products, arithmetic and copies ran while one was open for 5% of the time, Pallas kernels for 20%

profile of v1, /device:TPU:33, one launch (start us, length us, event | category | flops | bytes accessed | tf_op | source)
XLA Modules:
  0.0 116.9 jit_solution(16298948542065760885)
XLA Ops:
  0.0 0.9 copy.13
  1.0 0.9 maximum_maximum_fusion.refs_0_
  1.9 1.3 %collective-permute-start = (bf16[128,640]{1,0:T(8,128)(2,1)S(1)}, bf16[128,640]{1,0:T(8,128)(2,1)S(1)}, u32[]{:S(2)}, u32[]{:S(2)}) collective-permute-start(bf16[128,640]{1,0:T(8,128)(2,1)S(1)} %maximum_maximum_fusion.refs_0_), channel_id=1, source_target_pairs={{0,2},{2,4},{4,6},{6,0},{1,3},{3,5},{5,7},{7,1},{8,10},{10,12},{12... | collective-permute-start | bytes 491528 | tf_op jit(solution)/shard_map/ppermute | solution.py:42
  3.2 2.5 %collective-permute-start.1 = (bf16[128,640]{1,0:T(8,128)(2,1)S(1)}, bf16[128,640]{1,0:T(8,128)(2,1)S(1)}, u32[]{:S(2)}, u32[]{:S(2)}) collective-permute-start(bf16[128,640]{1,0:T(8,128)(2,1)S(1)} %maximum_maximum_fusion.refs_0_), channel_id=1, source_target_pairs={{0,4},{2,6},{4,0},{6,2},{1,5},{3,7},{5,1},{7,3},{8,12},{10,14},{12... | collective-permute-start | bytes 491528 | tf_op jit(solution)/shard_map/ppermute | solution.py:42
  5.6 1.2 collective-permute-start.2
  6.8 0.8 pad_maximum_fusion.1
  7.6 0.8 broadcast_in_dim.43
  8.4 8.0 %all-to-all-start = ((bf16[8,16,2048]{2,1,0:T(8,128)(2,1)}), bf16[8,16,2048]{2,1,0:T(8,128)(2,1)S(1)}, u32[]{:S(2)}, u32[]{:S(2)}) async-start(bf16[8,16,2048]{2,1,0:T(8,128)(2,1)} %broadcast_in_dim.43), calls=%async_computation | async-start | bytes 1048576 | tf_op jit(solution)/shard_map/all_to_all | solution.py:32
  16.5 0.1 select_select_fusion.1
  16.7 3.3 %collective-permute-start.5 = (bf16[256,640]{1,0:T(8,128)(2,1)S(1)}, bf16[256,640]{1,0:T(8,128)(2,1)S(1)}, u32[]{:S(2)}, u32[]{:S(2)}) collective-permute-start(bf16[256,640]{1,0:T(8,128)(2,1)S(1)} %pad_maximum_fusion), channel_id=1, source_target_pairs={{0,8},{8,16},{16,24},{24,32},{32,40},{40,48},{48,56},{56,64},{64,7... | collective-permute-start | bytes 983048 | tf_op jit(solution)/shard_map/ppermute | solution.py:37
  20.0 0.1 add_add_fusion.3.at_ref
  20.1 0.1 select_reduce_fusion.1
  20.2 0.4 select_reduce_fusion
  20.6 16.1 %collective-permute-done.5.refs_4_ = bf16[256,640]{1,0:T(8,128)(2,1)S(1)} collective-permute-done((bf16[256,640]{1,0:T(8,128)(2,1)S(1)}, bf16[256,640]{1,0:T(8,128)(2,1)S(1)}, u32[]{:S(2)}, u32[]{:S(2)}) %collective-permute-start.5) | collective-permute-done | bytes 327712 | tf_op jit(solution)/shard_map/ppermute | solution.py:37
  36.8 2.5 %collective-permute-start.6 = (bf16[768,640]{1,0:T(8,128)(2,1)S(1)}, bf16[768,640]{1,0:T(8,128)(2,1)}, u32[]{:S(2)}, u32[]{:S(2)}) collective-permute-start(bf16[768,640]{1,0:T(8,128)(2,1)S(1)} %joined.1.mine_ref), channel_id=1, source_target_pairs={{0,1},{1,0},{2,3},{3,2},{4,5},{5,4},{6,7},{7,6},{8,9},{9,8},{10,11... | collective-permute-start | bytes 2949128 | tf_op jit(solution)/shard_map/ppermute | solution.py:46
  39.2 1.0 constant_dynamic-slice_fusion
  40.2 0.2 collective-permute-start.3
  40.6 0.4 collective-permute-start.8
  41.0 2.3 %collective-permute-start.9 = (bf16[128,2048]{1,0:T(8,128)(2,1)S(1)}, bf16[128,2048]{1,0:T(8,128)(2,1)}, u32[]{:S(2)}, u32[]{:S(2)}) collective-permute-start(bf16[128,2048]{1,0:T(8,128)(2,1)S(1)} %bitcast.13), channel_id=1, source_target_pairs={{0,24},{8,0},{16,8},{24,16},{1,25},{9,1},{17,9},{25,17},{2,26},{10... | collective-permute-start | bytes 1572872 | tf_op jit(solution)/shard_map/ppermute | solution.py:42
  43.4 9.0 %collective-permute-done.3.q0_ref = bf16[128,1536]{1,0:T(8,128)(2,1)S(1)} collective-permute-done((bf16[128,1536]{1,0:T(8,128)(2,1)S(1)}, bf16[128,1536]{1,0:T(8,128)(2,1)S(1)}, u32[]{:S(2)}, u32[]{:S(2)}) %collective-permute-start.3) | collective-permute-done | bytes 393248 | tf_op jit(solution)/shard_map/ppermute | solution.py:272
  52.4 1.0 collective-permute-start.4
  53.5 0.2 copy.14.start_ref
  53.9 1.5 %constant_dynamic-slice_fusion.2 = (bf16[128,1536]{1,0:T(8,128)(2,1)S(1)}, bf16[128,1536]{1,0:T(8,128)(2,1)S(1)}, bf16[128,1536]{1,0:T(8,128)(2,1)S(1)}, bf16[128,1536]{1,0:T(8,128)(2,1)S(1)}) fusion(bf16[128,12288]{1,0:T(8,128)(2,1)} %param.6, s32[]{:T(128)S(6)} %select_n.139, s32[]{:T(128)S(6)} %select_n.135, s32[]{:T(128)S(6)} %select_n.134, s32[]{:T(128)S(6)} %select_n.138), kind=kLoop, calls=%fused_computation.16 | loop fusion | bytes 3145744 | tf_op jit(solution)/shard_map/dynamic_slice | solution.py:269
  55.4 10.2 %collective-permute-done.4.q1_ref = bf16[128,1536]{1,0:T(8,128)(2,1)S(1)} collective-permute-done((bf16[128,1536]{1,0:T(8,128)(2,1)}, bf16[128,1536]{1,0:T(8,128)(2,1)S(1)}, u32[]{:S(2)}, u32[]{:S(2)}) %collective-permute-start.4) | collective-permute-done | bytes 393248 | tf_op jit(solution)/shard_map/ppermute | solution.py:272
  65.6 0.5 collective-permute-start.16
  66.1 0.3 collective-permute-done.7.refs_1_
  66.3 3.5 %collective-permute-start.17 = (bf16[128,1536]{1,0:T(8,128)(2,1)S(1)}, bf16[128,1536]{1,0:T(8,128)(2,1)S(1)}, u32[]{:S(2)}, u32[]{:S(2)}) collective-permute-start(bf16[128,1536]{1,0:T(8,128)(2,1)S(1)} %get-tuple-element.31), channel_id=1, source_target_pairs={{0,7},{1,6},{2,1},{3,0},{4,3},{5,2},{6,5},{7,4},{8,15},{9,14},{10,... | collective-permute-start | bytes 1179656 | tf_op jit(solution)/shard_map/ppermute | solution.py:272
  69.9 0.2 collective-permute-start.13
  70.1 0.2 collective-permute-start.20
  70.3 5.6 %project.1 = (bf16[1536,2048]{1,0:T(8,128)(2,1)S(1)}, bf16[1536,1024]{1,0:T(8,128)(2,1)S(1)}) custom-call(s32[3]{0:T(128)S(1)} %pad_add_fusion.at_ref, bf16[768,640]{1,0:T(8,128)(2,1)S(1)} %joined.1.mine_ref, bf16[768,640]{1,0:T(8,128)(2,1)} %collective-permute-done.6.other_ref, bf16[128,2048]{1,0:T(8,128)(2,1)S(1)} %bitcast.14, ...), custom_call_target="tpu_custom_call" | custom-call | flops 3221225472 | bytes 12582912 | tf_op jit(solution)/shard_map/project/pallas_call | solution.py:136
  75.9 4.3 %attend.4 = (bf16[128,1024]{1,0:T(8,128)(2,1)S(1)}, bf16[128,1024]{1,0:T(8,128)(2,1)S(1)}) custom-call(s32[3]{0:T(128)S(1)} %add_add_fusion.at_ref, bf16[128,1536]{1,0:T(8,128)(2,1)S(1)} %collective-permute-done.3.q0_ref, bf16[128,1536]{1,0:T(8,128)(2,1)S(1)} %collective-permute-done.4.q1_ref, bf16[1536,2048]{1,0:T(8,128)(2,1)S(1)} %get-tuple-element.17.k_ref, ...), custom_call_target="tpu_custom_call" | custom-call | flops 1207959552 | bytes 4194304 | tf_op jit(solution)/shard_map/attend/pallas_call | solution.py:212
  80.2 3.9 %collective-permute-start.10 = (bf16[128,1024]{1,0:T(8,128)(2,1)S(1)}, bf16[128,1024]{1,0:T(8,128)(2,1)S(1)}, u32[]{:S(2)}, u32[]{:S(2)}) collective-permute-start(bf16[128,1024]{1,0:T(8,128)(2,1)S(1)} %get-tuple-element.19), channel_id=1, source_target_pairs={{4,0},{5,1},{6,2},{7,3},{0,4},{1,5},{2,6},{3,7},{12,8},{13,9},{14,... | collective-permute-start | bytes 786440 | tf_op jit(solution)/shard_map/ppermute | solution.py:295
  84.1 1.3 %collective-permute-done.17.q1_ref = bf16[128,1536]{1,0:T(8,128)(2,1)S(1)} collective-permute-done((bf16[128,1536]{1,0:T(8,128)(2,1)S(1)}, bf16[128,1536]{1,0:T(8,128)(2,1)S(1)}, u32[]{:S(2)}, u32[]{:S(2)}) %collective-permute-start.17) | collective-permute-done | bytes 393248 | tf_op jit(solution)/shard_map/ppermute | solution.py:272
  85.5 4.3 %attend.6 = (bf16[128,1024]{1,0:T(8,128)(2,1)S(1)}, bf16[128,1024]{1,0:T(8,128)(2,1)S(1)}) custom-call(s32[3]{0:T(128)S(1)} %add_add_fusion.2.at_ref, bf16[128,1536]{1,0:T(8,128)(2,1)S(1)} %collective-permute-done.16.q0_ref, bf16[128,1536]{1,0:T(8,128)(2,1)S(1)} %collective-permute-done.17.q1_ref, bf16[1536,2048]{1,0:T(8,128)(2,1)S(1)} %get-tuple-element.17.k_ref, ...), custom_call_target="tpu_custom_call" | custom-call | flops 1207959552 | bytes 4194304 | tf_op jit(solution)/shard_map/attend/pallas_call | solution.py:212
  89.8 0.4 collective-permute-start.18
  90.2 2.1 %collective-permute-start.11 = (bf16[128,1024]{1,0:T(8,128)(2,1)S(1)}, bf16[128,1024]{1,0:T(8,128)(2,1)S(1)}, u32[]{:S(2)}, u32[]{:S(2)}) collective-permute-start(bf16[128,1024]{1,0:T(8,128)(2,1)S(1)} %get-tuple-element.20), channel_id=1, source_target_pairs={{5,0},{4,1},{7,2},{6,3},{1,4},{0,5},{3,6},{2,7},{13,8},{12,9},{15,... | collective-permute-start | bytes 786440 | tf_op jit(solution)/shard_map/ppermute | solution.py:295
  92.3 3.5 %collective-permute-done.13.q1_ref = bf16[128,1536]{1,0:T(8,128)(2,1)S(1)} collective-permute-done((bf16[128,1536]{1,0:T(8,128)(2,1)S(1)}, bf16[128,1536]{1,0:T(8,128)(2,1)S(1)}, u32[]{:S(2)}, u32[]{:S(2)}) %collective-permute-start.13) | collective-permute-done | bytes 393248 | tf_op jit(solution)/shard_map/ppermute | solution.py:272
  95.9 4.3 %attend.5 = (bf16[128,1024]{1,0:T(8,128)(2,1)S(1)}, bf16[128,1024]{1,0:T(8,128)(2,1)S(1)}) custom-call(s32[3]{0:T(128)S(1)} %add_add_fusion.1.at_ref, bf16[128,1536]{1,0:T(8,128)(2,1)S(1)} %collective-permute-done.12.q0_ref, bf16[128,1536]{1,0:T(8,128)(2,1)S(1)} %collective-permute-done.13.q1_ref, bf16[1536,2048]{1,0:T(8,128)(2,1)S(1)} %get-tuple-element.17.k_ref, ...), custom_call_target="tpu_custom_call" | custom-call | flops 1207959552 | bytes 4194304 | tf_op jit(solution)/shard_map/attend/pallas_call | solution.py:212
  100.2 0.1 collective-permute-start.14
  100.3 0.1 collective-permute-start.15
  100.4 4.3 %attend.7 = (bf16[128,1024]{1,0:T(8,128)(2,1)S(1)}, bf16[128,1024]{1,0:T(8,128)(2,1)S(1)}) custom-call(s32[3]{0:T(128)S(1)} %add_add_fusion.3.at_ref, bf16[128,1536]{1,0:T(8,128)(2,1)S(1)} %get-tuple-element.28.q0_ref, bf16[128,1536]{1,0:T(8,128)(2,1)S(1)} %collective-permute-done.20.q1_ref, bf16[1536,2048]{1,0:T(8,128)(2,1)S(1)} %get-tuple-element.17.k_ref, ...), custom_call_target="tpu_custom_call" | custom-call | flops 1207959552 | bytes 4194304 | tf_op jit(solution)/shard_map/attend/pallas_call | solution.py:212
  104.7 2.4 %collective-permute-start.19 = (bf16[128,1024]{1,0:T(8,128)(2,1)S(1)}, bf16[128,1024]{1,0:T(8,128)(2,1)S(1)}, u32[]{:S(2)}, u32[]{:S(2)}) collective-permute-start(bf16[128,1024]{1,0:T(8,128)(2,1)S(1)} %get-tuple-element.24), channel_id=1, source_target_pairs={{7,0},{6,1},{1,2},{0,3},{3,4},{2,5},{5,6},{4,7},{15,8},{14,9},{9,1... | collective-permute-start | bytes 786440 | tf_op jit(solution)/shard_map/ppermute | solution.py:295
  107.1 0.2 broadcast_in_dim.28
  107.4 0.3 collective-permute-start.21
  107.7 6.5 %collective-permute-done.15 = bf16[128,1024]{1,0:T(8,128)(2,1)S(1)} collective-permute-done((bf16[128,1024]{1,0:T(8,128)(2,1)S(1)}, bf16[128,1024]{1,0:T(8,128)(2,1)S(1)}, u32[]{:S(2)}, u32[]{:S(2)}) %collective-permute-start.15) | collective-permute-done | bytes 262176 | tf_op jit(solution)/shard_map/ppermute | solution.py:295
  114.3 0.5 collective-permute-done.19
  114.9 1.3 %copy-done.1 = bf16[128,8192]{1,0:T(8,128)(2,1)} copy-done((bf16[128,8192]{1,0:T(8,128)(2,1)}, bf16[128,8192]{1,0:T(8,128)(2,1)S(1)}, u32[]{:S(2)}) %copy-start.1) | copy-done | bytes 2097176
  116.2 0.7 constant_dynamic-update-slice_fusion
  (43 shorter events, 0.8 us)
Async XLA Ops:
  0.0 16.5 %copy-start.2 = (bf16[128,512]{1,0:T(8,128)(2,1)S(1)}, bf16[128,512]{1,0:T(8,128)(2,1)}, u32[]{:S(2)}) copy-start(bf16[128,512]{1,0:T(8,128)(2,1)} %param.7) | copy-start | bytes 393220
  0.0 20.1 %copy-start.4 = (s32[128]{0:T(128)S(1)}, s32[128]{0:T(128)}, u32[]{:S(2)}) copy-start(s32[128]{0:T(128)} %param.11) | copy-start | bytes 1540
  1.9 14.5 %collective-permute-start = (bf16[128,640]{1,0:T(8,128)(2,1)S(1)}, bf16[128,640]{1,0:T(8,128)(2,1)S(1)}, u32[]{:S(2)}, u32[]{:S(2)}) collective-permute-start(bf16[128,640]{1,0:T(8,128)(2,1)S(1)} %maximum_maximum_fusion.refs_0_), channel_id=1, source_target_pairs={{0,2},{2,4},{4,6},{6,0},{1,3},{3,5},{5,7},{7,1},{8,10},{10,12},{12... | collective-permute-start | bytes 491528 | tf_op jit(solution)/shard_map/ppermute | solution.py:42
  3.2 13.3 %collective-permute-start.1 = (bf16[128,640]{1,0:T(8,128)(2,1)S(1)}, bf16[128,640]{1,0:T(8,128)(2,1)S(1)}, u32[]{:S(2)}, u32[]{:S(2)}) collective-permute-start(bf16[128,640]{1,0:T(8,128)(2,1)S(1)} %maximum_maximum_fusion.refs_0_), channel_id=1, source_target_pairs={{0,4},{2,6},{4,0},{6,2},{1,5},{3,7},{5,1},{7,3},{8,12},{10,14},{12... | collective-permute-start | bytes 491528 | tf_op jit(solution)/shard_map/ppermute | solution.py:42
  5.6 10.8 %collective-permute-start.2 = (bf16[128,640]{1,0:T(8,128)(2,1)S(1)}, bf16[128,640]{1,0:T(8,128)(2,1)S(1)}, u32[]{:S(2)}, u32[]{:S(2)}) collective-permute-start(bf16[128,640]{1,0:T(8,128)(2,1)S(1)} %maximum_maximum_fusion.refs_0_), channel_id=1, source_target_pairs={{0,6},{2,0},{4,2},{6,4},{1,7},{3,1},{5,3},{7,5},{8,14},{10,8},{12,... | collective-permute-start | bytes 491528 | tf_op jit(solution)/shard_map/ppermute | solution.py:42
  8.4 32.1 %all-to-all-start = ((bf16[8,16,2048]{2,1,0:T(8,128)(2,1)}), bf16[8,16,2048]{2,1,0:T(8,128)(2,1)S(1)}, u32[]{:S(2)}, u32[]{:S(2)}) async-start(bf16[8,16,2048]{2,1,0:T(8,128)(2,1)} %broadcast_in_dim.43), calls=%async_computation | async-start | bytes 1048576 | tf_op jit(solution)/shard_map/all_to_all | solution.py:32
  16.4 22.8 %copy-start = (bf16[128,12288]{1,0:T(8,128)(2,1)S(1)}, bf16[128,12288]{1,0:T(8,128)(2,1)}, u32[]{:S(2)}) copy-start(bf16[128,12288]{1,0:T(8,128)(2,1)} %param.6) | copy-start | bytes 9437188
  16.7 20.0 %collective-permute-start.5 = (bf16[256,640]{1,0:T(8,128)(2,1)S(1)}, bf16[256,640]{1,0:T(8,128)(2,1)S(1)}, u32[]{:S(2)}, u32[]{:S(2)}) collective-permute-start(bf16[256,640]{1,0:T(8,128)(2,1)S(1)} %pad_maximum_fusion), channel_id=1, source_target_pairs={{0,8},{8,16},{16,24},{24,32},{32,40},{40,48},{48,56},{56,64},{64,7... | collective-permute-start | bytes 983048 | tf_op jit(solution)/shard_map/ppermute | solution.py:37
  36.8 33.3 %collective-permute-start.6 = (bf16[768,640]{1,0:T(8,128)(2,1)S(1)}, bf16[768,640]{1,0:T(8,128)(2,1)}, u32[]{:S(2)}, u32[]{:S(2)}) collective-permute-start(bf16[768,640]{1,0:T(8,128)(2,1)S(1)} %joined.1.mine_ref), channel_id=1, source_target_pairs={{0,1},{1,0},{2,3},{3,2},{4,5},{5,4},{6,7},{7,6},{8,9},{9,8},{10,11... | collective-permute-start | bytes 2949128 | tf_op jit(solution)/shard_map/ppermute | solution.py:46
  40.2 12.1 %collective-permute-start.3 = (bf16[128,1536]{1,0:T(8,128)(2,1)S(1)}, bf16[128,1536]{1,0:T(8,128)(2,1)S(1)}, u32[]{:S(2)}, u32[]{:S(2)}) collective-permute-start(bf16[128,1536]{1,0:T(8,128)(2,1)S(1)} %get-tuple-element.30), channel_id=1, source_target_pairs={{0,4},{1,5},{2,6},{3,7},{4,0},{5,1},{6,2},{7,3},{8,12},{9,13},{10,... | collective-permute-start | bytes 1179656 | tf_op jit(solution)/shard_map/ppermute | solution.py:272
  40.6 25.8 %collective-permute-start.7 = (bf16[128,2048]{1,0:T(8,128)(2,1)S(1)}, bf16[128,2048]{1,0:T(8,128)(2,1)}, u32[]{:S(2)}, u32[]{:S(2)}) collective-permute-start(bf16[128,2048]{1,0:T(8,128)(2,1)S(1)} %bitcast.11), channel_id=1, source_target_pairs={{0,8},{8,16},{16,24},{24,0},{1,9},{9,17},{17,25},{25,1},{2,10},{10... | collective-permute-start | bytes 1572872 | tf_op jit(solution)/shard_map/ppermute | solution.py:42
  40.6 29.2 %collective-permute-start.8 = (bf16[128,2048]{1,0:T(8,128)(2,1)S(1)}, bf16[128,2048]{1,0:T(8,128)(2,1)}, u32[]{:S(2)}, u32[]{:S(2)}) collective-permute-start(bf16[128,2048]{1,0:T(8,128)(2,1)S(1)} %bitcast.12), channel_id=1, source_target_pairs={{0,16},{8,24},{16,0},{24,8},{1,17},{9,25},{17,1},{25,9},{2,18},{10... | collective-permute-start | bytes 1572872 | tf_op jit(solution)/shard_map/ppermute | solution.py:42
  41.0 28.9 %collective-permute-start.9 = (bf16[128,2048]{1,0:T(8,128)(2,1)S(1)}, bf16[128,2048]{1,0:T(8,128)(2,1)}, u32[]{:S(2)}, u32[]{:S(2)}) collective-permute-start(bf16[128,2048]{1,0:T(8,128)(2,1)S(1)} %bitcast.13), channel_id=1, source_target_pairs={{0,24},{8,0},{16,8},{24,16},{1,25},{9,1},{17,9},{25,17},{2,26},{10... | collective-permute-start | bytes 1572872 | tf_op jit(solution)/shard_map/ppermute | solution.py:42
  52.4 13.2 %collective-permute-start.4 = (bf16[128,1536]{1,0:T(8,128)(2,1)}, bf16[128,1536]{1,0:T(8,128)(2,1)S(1)}, u32[]{:S(2)}, u32[]{:S(2)}) collective-permute-start(bf16[128,1536]{1,0:T(8,128)(2,1)} %get-tuple-element.29), channel_id=1, source_target_pairs={{0,5},{1,4},{2,7},{3,6},{4,1},{5,0},{6,3},{7,2},{8,13},{9,12},{10,... | collective-permute-start | bytes 1179656 | tf_op jit(solution)/shard_map/ppermute | solution.py:272
  53.8 16.3 %copy-start.3 = (bf16[128,1536]{1,0:T(8,128)(2,1)S(1)}, bf16[128,1536]{1,0:T(8,128)(2,1)}, u32[]{:S(2)}) copy-start(bf16[128,1536]{1,0:T(8,128)(2,1)} %get-tuple-element.27) | copy-start | bytes 1179652
  65.6 14.6 %collective-permute-start.16 = (bf16[128,1536]{1,0:T(8,128)(2,1)S(1)}, bf16[128,1536]{1,0:T(8,128)(2,1)S(1)}, u32[]{:S(2)}, u32[]{:S(2)}) collective-permute-start(bf16[128,1536]{1,0:T(8,128)(2,1)S(1)} %get-tuple-element.34), channel_id=1, source_target_pairs={{0,6},{1,7},{2,0},{3,1},{4,2},{5,3},{6,4},{7,5},{8,14},{9,15},{10,... | collective-permute-start | bytes 1179656 | tf_op jit(solution)/shard_map/ppermute | solution.py:272
  66.3 19.1 %collective-permute-start.17 = (bf16[128,1536]{1,0:T(8,128)(2,1)S(1)}, bf16[128,1536]{1,0:T(8,128)(2,1)S(1)}, u32[]{:S(2)}, u32[]{:S(2)}) collective-permute-start(bf16[128,1536]{1,0:T(8,128)(2,1)S(1)} %get-tuple-element.31), channel_id=1, source_target_pairs={{0,7},{1,6},{2,1},{3,0},{4,3},{5,2},{6,5},{7,4},{8,15},{9,14},{10,... | collective-permute-start | bytes 1179656 | tf_op jit(solution)/shard_map/ppermute | solution.py:272
  69.9 20.3 %collective-permute-start.12 = (bf16[128,1536]{1,0:T(8,128)(2,1)S(1)}, bf16[128,1536]{1,0:T(8,128)(2,1)S(1)}, u32[]{:S(2)}, u32[]{:S(2)}) collective-permute-start(bf16[128,1536]{1,0:T(8,128)(2,1)S(1)} %get-tuple-element.33), channel_id=1, source_target_pairs={{0,2},{1,3},{2,4},{3,5},{4,6},{5,7},{6,0},{7,1},{8,10},{9,11},{10,... | collective-permute-start | bytes 1179656 | tf_op jit(solution)/shard_map/ppermute | solution.py:272
  69.9 26.0 %collective-permute-start.13 = (bf16[128,1536]{1,0:T(8,128)(2,1)S(1)}, bf16[128,1536]{1,0:T(8,128)(2,1)S(1)}, u32[]{:S(2)}, u32[]{:S(2)}) collective-permute-start(bf16[128,1536]{1,0:T(8,128)(2,1)S(1)} %get-tuple-element.32), channel_id=1, source_target_pairs={{0,3},{1,2},{2,5},{3,4},{4,7},{5,6},{6,1},{7,0},{8,11},{9,10},{10,... | collective-permute-start | bytes 1179656 | tf_op jit(solution)/shard_map/ppermute | solution.py:272
  70.1 30.2 %collective-permute-start.20 = (bf16[128,1536]{1,0:T(8,128)(2,1)S(1)}, bf16[128,1536]{1,0:T(8,128)(2,1)S(1)}, u32[]{:S(2)}, u32[]{:S(2)}) collective-permute-start(bf16[128,1536]{1,0:T(8,128)(2,1)S(1)} %copy-done.3), channel_id=1, source_target_pairs={{0,1},{1,0},{2,3},{3,2},{4,5},{5,4},{6,7},{7,6},{8,9},{9,8},{10,11... | collective-permute-start | bytes 1179656 | tf_op jit(solution)/shard_map/ppermute | solution.py:272
  80.2 24.5 %collective-permute-start.10 = (bf16[128,1024]{1,0:T(8,128)(2,1)S(1)}, bf16[128,1024]{1,0:T(8,128)(2,1)S(1)}, u32[]{:S(2)}, u32[]{:S(2)}) collective-permute-start(bf16[128,1024]{1,0:T(8,128)(2,1)S(1)} %get-tuple-element.19), channel_id=1, source_target_pairs={{4,0},{5,1},{6,2},{7,3},{0,4},{1,5},{2,6},{3,7},{12,8},{13,9},{14,... | collective-permute-start | bytes 786440 | tf_op jit(solution)/shard_map/ppermute | solution.py:295
  89.8 24.4 %collective-permute-start.18 = (bf16[128,1024]{1,0:T(8,128)(2,1)S(1)}, bf16[128,1024]{1,0:T(8,128)(2,1)S(1)}, u32[]{:S(2)}, u32[]{:S(2)}) collective-permute-start(bf16[128,1024]{1,0:T(8,128)(2,1)S(1)} %get-tuple-element.23), channel_id=1, source_target_pairs={{6,0},{7,1},{0,2},{1,3},{2,4},{3,5},{4,6},{5,7},{14,8},{15,9},{8,1... | collective-permute-start | bytes 786440 | tf_op jit(solution)/shard_map/ppermute | solution.py:295
  90.2 17.2 %collective-permute-start.11 = (bf16[128,1024]{1,0:T(8,128)(2,1)S(1)}, bf16[128,1024]{1,0:T(8,128)(2,1)S(1)}, u32[]{:S(2)}, u32[]{:S(2)}) collective-permute-start(bf16[128,1024]{1,0:T(8,128)(2,1)S(1)} %get-tuple-element.20), channel_id=1, source_target_pairs={{5,0},{4,1},{7,2},{6,3},{1,4},{0,5},{3,6},{2,7},{13,8},{12,9},{15,... | collective-permute-start | bytes 786440 | tf_op jit(solution)/shard_map/ppermute | solution.py:295
  100.2 7.5 %collective-permute-start.14 = (bf16[128,1024]{1,0:T(8,128)(2,1)S(1)}, bf16[128,1024]{1,0:T(8,128)(2,1)S(1)}, u32[]{:S(2)}, u32[]{:S(2)}) collective-permute-start(bf16[128,1024]{1,0:T(8,128)(2,1)S(1)} %get-tuple-element.21), channel_id=1, source_target_pairs={{2,0},{3,1},{4,2},{5,3},{6,4},{7,5},{0,6},{1,7},{10,8},{11,9},{12,... | collective-permute-start | bytes 786440 | tf_op jit(solution)/shard_map/ppermute | solution.py:295
  100.3 13.9 %collective-permute-start.15 = (bf16[128,1024]{1,0:T(8,128)(2,1)S(1)}, bf16[128,1024]{1,0:T(8,128)(2,1)S(1)}, u32[]{:S(2)}, u32[]{:S(2)}) collective-permute-start(bf16[128,1024]{1,0:T(8,128)(2,1)S(1)} %get-tuple-element.22), channel_id=1, source_target_pairs={{3,0},{2,1},{5,2},{4,3},{7,4},{6,5},{1,6},{0,7},{11,8},{10,9},{13,... | collective-permute-start | bytes 786440 | tf_op jit(solution)/shard_map/ppermute | solution.py:295
  104.7 10.1 %collective-permute-start.19 = (bf16[128,1024]{1,0:T(8,128)(2,1)S(1)}, bf16[128,1024]{1,0:T(8,128)(2,1)S(1)}, u32[]{:S(2)}, u32[]{:S(2)}) collective-permute-start(bf16[128,1024]{1,0:T(8,128)(2,1)S(1)} %get-tuple-element.24), channel_id=1, source_target_pairs={{7,0},{6,1},{1,2},{0,3},{3,4},{2,5},{5,6},{4,7},{15,8},{14,9},{9,1... | collective-permute-start | bytes 786440 | tf_op jit(solution)/shard_map/ppermute | solution.py:295
  107.4 7.5 %collective-permute-start.21 = (bf16[128,1024]{1,0:T(8,128)(2,1)S(1)}, bf16[128,1024]{1,0:T(8,128)(2,1)S(1)}, u32[]{:S(2)}, u32[]{:S(2)}) collective-permute-start(bf16[128,1024]{1,0:T(8,128)(2,1)S(1)} %get-tuple-element.26), channel_id=1, source_target_pairs={{1,0},{0,1},{3,2},{2,3},{5,4},{4,5},{7,6},{6,7},{9,8},{8,9},{11,10... | collective-permute-start | bytes 786440 | tf_op jit(solution)/shard_map/ppermute | solution.py:295
  114.8 1.3 %copy-start.1 = (bf16[128,8192]{1,0:T(8,128)(2,1)}, bf16[128,8192]{1,0:T(8,128)(2,1)S(1)}, u32[]{:S(2)}) copy-start(bf16[128,8192]{1,0:T(8,128)(2,1)S(1)} %constant_dynamic-update-slice_fusion.1) | copy-start | bytes 6291460

commit v2 on v1

--- a/solution.py
+++ b/solution.py
@@ -15,11 +15,11 @@
 VDIM = 128
 WIDE = 256
 SUB = 128
-HALO = 512
+HALO = 256
 SEQ = ("z", "y")
 GROUP = ("x", "c")
 EVERY = ("z", "y", "x", "c")
-CHUNK = 512
+CHUNK = 640
 STRIP = 16
 VMEM_LIMIT = 24 * 2**20
 INTERPRET = False
@@ -224,7 +224,7 @@
         ],
         compiler_params=pltpu.CompilerParams(vmem_limit_bytes=VMEM_LIMIT),
         cost_estimate=pl.CostEstimate(
-            flops=4 * heads * rows * window * (WIDE + VDIM),
+            flops=40 * heads * rows * window * (WIDE + VDIM),
             bytes_accessed=4 * rows * heads * 1024,
             transcendentals=2 * heads * rows * window,
         ),

time: 117 us -> 131 us (1.12)
  waiting for transfers between devices: 47.5 us -> 68.6 us
  Pallas kernels: 22.9 us -> 17.5 us
  starting transfers between devices: 36.4 us -> 32.9 us
  local copies, waits for them, and re-layouts: 6.89 us -> 8.4 us
    ppermute x6, waiting for transfers between devices: 0.26 us -> 20.6 us  [turned(): lax.ppermute(value, axis, [(i, (i + steps) % count) for i in range(count)])]
    ppermute x7, waiting for transfers between devices: 7 us -> 13.3 us  [whole(): back = lax.ppermute(back, GROUP, [(b, a) for a, b in hops(step, flip)])]
    ppermute x1, waiting for transfers between devices: 16.1 us -> 10 us  [shifted(): lax.ppermute(value, axes, [(i, i + steps) for i in range(count - steps)])]
    ppermute x7, starting transfers between devices: 9.35 us -> 4.77 us  [whole(): back = lax.ppermute(back, GROUP, [(b, a) for a, b in hops(step, flip)])]
    pallas_call x4, Pallas kernels: 17.3 us -> 12.9 us  [attend(): pl.pallas_call(functools.partial(attend_kernel, score_scale), in_specs=[I...]
    dynamic_slice x2, local copies, waits for them, and re-layouts: 2.5 us -> 4.04 us  [sent(): lax.dynamic_slice_in_dim(queries if step % 2 else late, width * block_of(...]
  transfers between devices with their start and end apart: 23 -> 23, of which waited for: 8 -> 7; matrix products, arithmetic and copies ran while one was open for 5% -> 6% of each run, Pallas kernels for 20% -> 13%
where the time goes in v2:
time: 131 us; the launch traced here: 130 us
  waiting for transfers between devices  68.6 us (52%)
  starting transfers between devices  32.9 us (25%)
  Pallas kernels  17.5 us (13%)
  local copies, waits for them, and re-layouts  8.4 us (6%)
  other arithmetic  2.7 us (2%)
    ppermute x7, waiting for transfers between devices, sent(): return lax.ppermute(out, GROUP, hops(step, flip))  24.7 us
    ppermute x6, waiting for transfers between devices, turned(): lax.ppermute(value, axis, [(i, (i + steps) % count) for i in range(count)])  20.6 us
    ppermute x7, waiting for transfers between devices, whole(): back = lax.ppermute(back, GROUP, [(b, a) for a, b in hops(step, flip)])  13.3 us
    pallas_call x4, Pallas kernels, attend(): pl.pallas_call(functools.partial(attend_kernel, score_scale), in_specs=[I...  12.9 us
    ppermute x1, waiting for transfers between devices, shifted(): lax.ppermute(value, axes, [(i, i + steps) for i in range(count - steps)])  10 us
    all_to_all x1, starting transfers between devices, spread(): return lax.all_to_all(copies, axis, 0, 0)  8.14 us
    ppermute x6, starting transfers between devices, turned(): lax.ppermute(value, axis, [(i, (i + steps) % count) for i in range(count)])  7.64 us
    ppermute x7, starting transfers between devices, sent(): return lax.ppermute(out, GROUP, hops(step, flip))  6.09 us
  transfers between devices with their start and end apart: 23, of which 7 were waited for; matrix products, arithmetic and copies ran while one was open for 6% of the time, Pallas kernels for 13%

profile of v2, /device:TPU:33, one launch (start us, length us, event | category | flops | bytes accessed | tf_op | source)
XLA Modules:
  0.0 130.4 jit_solution(7481996808155279321)
XLA Ops:
  0.0 0.8 copy.13
  0.8 0.1 pad.16.clone
  0.9 0.9 maximum_maximum_fusion.refs_0_
  1.9 1.3 collective-permute-start
  3.1 2.5 %collective-permute-start.1 = (bf16[128,640]{1,0:T(8,128)(2,1)S(1)}, bf16[128,640]{1,0:T(8,128)(2,1)S(1)}, u32[]{:S(2)}, u32[]{:S(2)}) collective-permute-start(bf16[128,640]{1,0:T(8,128)(2,1)S(1)} %maximum_maximum_fusion.refs_0_), channel_id=1, source_target_pairs={{0,4},{2,6},{4,0},{6,2},{1,5},{3,7},{5,1},{7,3},{8,12},{10,14},{12... | collective-permute-start | bytes 491528 | tf_op jit(solution)/shard_map/ppermute | solution.py:42
  5.6 1.2 collective-permute-start.2
  6.8 0.8 pad_maximum_fusion
  7.5 0.8 broadcast_in_dim.43
  8.4 8.1 %all-to-all-start = ((bf16[8,16,2048]{2,1,0:T(8,128)(2,1)}), bf16[8,16,2048]{2,1,0:T(8,128)(2,1)S(1)}, u32[]{:S(2)}, u32[]{:S(2)}) async-start(bf16[8,16,2048]{2,1,0:T(8,128)(2,1)} %broadcast_in_dim.43), calls=%async_computation | async-start | bytes 1048576 | tf_op jit(solution)/shard_map/all_to_all | solution.py:32
  16.5 2.6 %constant_dynamic-slice_fusion.2 = (bf16[128,1536]{1,0:T(8,128)(2,1)}, bf16[128,1536]{1,0:T(8,128)(2,1)}, bf16[128,1536]{1,0:T(8,128)(2,1)}, bf16[128,1536]{1,0:T(8,128)(2,1)}) fusion(bf16[128,12288]{1,0:T(8,128)(2,1)} %param.6, s32[]{:T(128)S(6)} %select_n.103, s32[]{:T(128)S(6)} %select_n.99, s32[]{:T(128)S(6)} %select_n.98, s32[]{:T(128)S(6)} %select_n.102), kind=kLoop, calls=%fused_computation.14 | loop fusion | bytes 3145744 | tf_op jit(solution)/shard_map/dynamic_slice | solution.py:269
  19.1 0.1 select_select_fusion
  19.2 3.2 %collective-permute-start.5 = (bf16[128,640]{1,0:T(8,128)(2,1)S(1)}, bf16[128,640]{1,0:T(8,128)(2,1)S(1)}, u32[]{:S(2)}, u32[]{:S(2)}) collective-permute-start(bf16[128,640]{1,0:T(8,128)(2,1)S(1)} %select_select_fusion), channel_id=1, source_target_pairs={{0,8},{8,16},{16,24},{24,32},{32,40},{40,48},{48,56},{56,64},{64,7... | collective-permute-start | bytes 491528 | tf_op jit(solution)/shard_map/ppermute | solution.py:37
  22.4 0.1 add_add_fusion.3.at_ref
  22.5 10.0 %collective-permute-done.5.refs_4_ = bf16[128,640]{1,0:T(8,128)(2,1)S(1)} collective-permute-done((bf16[128,640]{1,0:T(8,128)(2,1)S(1)}, bf16[128,640]{1,0:T(8,128)(2,1)S(1)}, u32[]{:S(2)}, u32[]{:S(2)}) %collective-permute-start.5) | collective-permute-done | bytes 163872 | tf_op jit(solution)/shard_map/ppermute | solution.py:37
  32.6 3.0 %collective-permute-start.6 = (bf16[640,640]{1,0:T(8,128)(2,1)S(1)}, bf16[640,640]{1,0:T(8,128)(2,1)S(1)}, u32[]{:S(2)}, u32[]{:S(2)}) collective-permute-start(bf16[640,640]{1,0:T(8,128)(2,1)S(1)} %joined.1.mine_ref), channel_id=1, source_target_pairs={{0,1},{1,0},{2,3},{3,2},{4,5},{5,4},{6,7},{7,6},{8,9},{9,8},{10,11... | collective-permute-start | bytes 2457608 | tf_op jit(solution)/shard_map/ppermute | solution.py:46
  35.7 0.1 select_reduce_fusion.1
  35.9 0.4 select_reduce_fusion
  36.3 0.1 collective-permute-start.7
  36.3 0.3 collective-permute-start.8
  36.6 2.4 %collective-permute-start.9 = (bf16[128,2048]{1,0:T(8,128)(2,1)S(1)}, bf16[128,2048]{1,0:T(8,128)(2,1)}, u32[]{:S(2)}, u32[]{:S(2)}) collective-permute-start(bf16[128,2048]{1,0:T(8,128)(2,1)S(1)} %bitcast.13), channel_id=1, source_target_pairs={{0,24},{8,0},{16,8},{24,16},{1,25},{9,1},{17,9},{25,17},{2,26},{10... | collective-permute-start | bytes 1572872 | tf_op jit(solution)/shard_map/ppermute | solution.py:42
  39.1 0.2 copy.14.start_ref
  39.4 0.1 add_add_fusion.at_ref
  39.6 0.6 collective-permute-start.17
  40.2 1.5 %constant_dynamic-slice_fusion = (bf16[128,1536]{1,0:T(8,128)(2,1)S(1)}, bf16[128,1536]{1,0:T(8,128)(2,1)S(1)}, bf16[128,1536]{1,0:T(8,128)(2,1)S(1)}, bf16[128,1536]{1,0:T(8,128)(2,1)S(1)}) fusion(bf16[128,12288]{1,0:T(8,128)(2,1)} %param.6, s32[]{:T(128)S(6)} %select_n.107, s32[]{:T(128)S(6)} %select_n.106, s32[]{:T(128)S(6)} %select_n.93, s32[]{:T(128)S(6)} %select_n.92), kind=kLoop, calls=%fused_computation.10 | loop fusion | bytes 3145744 | tf_op jit(solution)/shard_map/dynamic_slice | solution.py:269
  41.7 20.6 %collective-permute-done.7.refs_1_ = bf16[128,2048]{1,0:T(8,128)(2,1)S(1)} collective-permute-done((bf16[128,2048]{1,0:T(8,128)(2,1)S(1)}, bf16[128,2048]{1,0:T(8,128)(2,1)S(1)}, u32[]{:S(2)}, u32[]{:S(2)}) %collective-permute-start.7) | collective-permute-done | bytes 524320 | tf_op jit(solution)/shard_map/ppermute | solution.py:42
  62.2 0.3 collective-permute-start.12
  62.6 0.9 collective-permute-start.13
  63.4 0.6 collective-permute-start.20
  64.0 4.5 %project.1 = (bf16[1280,2048]{1,0:T(8,128)(2,1)S(1)}, bf16[1280,1024]{1,0:T(8,128)(2,1)S(1)}) custom-call(s32[3]{0:T(128)S(1)} %pad_add_fusion.at_ref, bf16[640,640]{1,0:T(8,128)(2,1)S(1)} %joined.1.mine_ref, bf16[640,640]{1,0:T(8,128)(2,1)S(1)} %collective-permute-done.6.other_ref, bf16[128,2048]{1,0:T(8,128)(2,1)S(1)} %bitcast.14, ...), custom_call_target="tpu_custom_call" | custom-call | flops 2684354560 | bytes 10485760 | tf_op jit(solution)/shard_map/project/pallas_call | solution.py:136
  68.5 3.2 %collective-permute-start.3 = (bf16[128,1536]{1,0:T(8,128)(2,1)S(1)}, bf16[128,1536]{1,0:T(8,128)(2,1)S(1)}, u32[]{:S(2)}, u32[]{:S(2)}) collective-permute-start(bf16[128,1536]{1,0:T(8,128)(2,1)S(1)} %get-tuple-element.30), channel_id=1, source_target_pairs={{0,4},{1,5},{2,6},{3,7},{4,0},{5,1},{6,2},{7,3},{8,12},{9,13},{10,... | collective-permute-start | bytes 1179656 | tf_op jit(solution)/shard_map/ppermute | solution.py:272
  71.8 0.5 collective-permute-start.4
  72.3 3.6 %attend.6 = (bf16[128,1024]{1,0:T(8,128)(2,1)S(1)}, bf16[128,1024]{1,0:T(8,128)(2,1)S(1)}) custom-call(s32[3]{0:T(128)S(1)} %add_add_fusion.2.at_ref, bf16[128,1536]{1,0:T(8,128)(2,1)} %collective-permute-done.16.q0_ref, bf16[128,1536]{1,0:T(8,128)(2,1)S(1)} %collective-permute-done.17.q1_ref, bf16[1280,2048]{1,0:T(8,128)(2,1)S(1)} %get-tuple-element.17.k_ref, ...), custom_call_target="tpu_custom_call" | custom-call | flops 8053063680 | bytes 4194304 | tf_op jit(solution)/shard_map/attend/pallas_call | solution.py:212
  75.9 0.4 collective-permute-start.18
  76.3 24.6 %collective-permute-done.13.q1_ref = bf16[128,1536]{1,0:T(8,128)(2,1)S(1)} collective-permute-done((bf16[128,1536]{1,0:T(8,128)(2,1)S(1)}, bf16[128,1536]{1,0:T(8,128)(2,1)S(1)}, u32[]{:S(2)}, u32[]{:S(2)}) %collective-permute-start.13) | collective-permute-done | bytes 393248 | tf_op jit(solution)/shard_map/ppermute | solution.py:272
  100.9 3.1 %attend.5 = (bf16[128,1024]{1,0:T(8,128)(2,1)S(1)}, bf16[128,1024]{1,0:T(8,128)(2,1)S(1)}) custom-call(s32[3]{0:T(128)S(1)} %add_add_fusion.1.at_ref, bf16[128,1536]{1,0:T(8,128)(2,1)S(1)} %collective-permute-done.12.q0_ref, bf16[128,1536]{1,0:T(8,128)(2,1)S(1)} %collective-permute-done.13.q1_ref, bf16[1280,2048]{1,0:T(8,128)(2,1)S(1)} %get-tuple-element.17.k_ref, ...), custom_call_target="tpu_custom_call" | custom-call | flops 8053063680 | bytes 4194304 | tf_op jit(solution)/shard_map/attend/pallas_call | solution.py:212
  104.0 0.1 collective-permute-start.14
  104.1 3.1 %attend.4 = (bf16[128,1024]{1,0:T(8,128)(2,1)S(1)}, bf16[128,1024]{1,0:T(8,128)(2,1)S(1)}) custom-call(s32[3]{0:T(128)S(1)} %add_add_fusion.at_ref, bf16[128,1536]{1,0:T(8,128)(2,1)S(1)} %collective-permute-done.3.q0_ref, bf16[128,1536]{1,0:T(8,128)(2,1)S(1)} %collective-permute-done.4.q1_ref, bf16[1280,2048]{1,0:T(8,128)(2,1)S(1)} %get-tuple-element.17.k_ref, ...), custom_call_target="tpu_custom_call" | custom-call | flops 8053063680 | bytes 4194304 | tf_op jit(solution)/shard_map/attend/pallas_call | solution.py:212
  107.2 0.1 collective-permute-start.10
  107.3 3.2 %collective-permute-start.11 = (bf16[128,1024]{1,0:T(8,128)(2,1)S(1)}, bf16[128,1024]{1,0:T(8,128)(2,1)S(1)}, u32[]{:S(2)}, u32[]{:S(2)}) collective-permute-start(bf16[128,1024]{1,0:T(8,128)(2,1)S(1)} %get-tuple-element.20), channel_id=1, source_target_pairs={{5,0},{4,1},{7,2},{6,3},{1,4},{0,5},{3,6},{2,7},{13,8},{12,9},{15,... | collective-permute-start | bytes 786440 | tf_op jit(solution)/shard_map/ppermute | solution.py:295
  110.6 1.0 collective-permute-start.15
  111.5 3.1 %attend.7 = (bf16[128,1024]{1,0:T(8,128)(2,1)S(1)}, bf16[128,1024]{1,0:T(8,128)(2,1)S(1)}) custom-call(s32[3]{0:T(128)S(1)} %add_add_fusion.3.at_ref, bf16[128,1536]{1,0:T(8,128)(2,1)S(1)} %get-tuple-element.28.q0_ref, bf16[128,1536]{1,0:T(8,128)(2,1)S(1)} %collective-permute-done.20.q1_ref, bf16[1280,2048]{1,0:T(8,128)(2,1)S(1)} %get-tuple-element.17.k_ref, ...), custom_call_target="tpu_custom_call" | custom-call | flops 8053063680 | bytes 4194304 | tf_op jit(solution)/shard_map/attend/pallas_call | solution.py:212
  114.7 1.9 %collective-permute-done.10 = bf16[128,1024]{1,0:T(8,128)(2,1)S(1)} collective-permute-done((bf16[128,1024]{1,0:T(8,128)(2,1)S(1)}, bf16[128,1024]{1,0:T(8,128)(2,1)S(1)}, u32[]{:S(2)}, u32[]{:S(2)}) %collective-permute-start.10) | collective-permute-done | bytes 262176 | tf_op jit(solution)/shard_map/ppermute | solution.py:295
  116.6 0.2 broadcast_in_dim.28
  116.8 6.2 %collective-permute-done.11 = bf16[128,1024]{1,0:T(8,128)(2,1)S(1)} collective-permute-done((bf16[128,1024]{1,0:T(8,128)(2,1)S(1)}, bf16[128,1024]{1,0:T(8,128)(2,1)S(1)}, u32[]{:S(2)}, u32[]{:S(2)}) %collective-permute-start.11) | collective-permute-done | bytes 262176 | tf_op jit(solution)/shard_map/ppermute | solution.py:295
  123.1 3.7 %collective-permute-done.15 = bf16[128,1024]{1,0:T(8,128)(2,1)S(1)} collective-permute-done((bf16[128,1024]{1,0:T(8,128)(2,1)S(1)}, bf16[128,1024]{1,0:T(8,128)(2,1)S(1)}, u32[]{:S(2)}, u32[]{:S(2)}) %collective-permute-start.15) | collective-permute-done | bytes 262176 | tf_op jit(solution)/shard_map/ppermute | solution.py:295
  126.8 1.5 %collective-permute-done.19 = bf16[128,1024]{1,0:T(8,128)(2,1)S(1)} collective-permute-done((bf16[128,1024]{1,0:T(8,128)(2,1)S(1)}, bf16[128,1024]{1,0:T(8,128)(2,1)S(1)}, u32[]{:S(2)}, u32[]{:S(2)}) %collective-permute-start.19) | collective-permute-done | bytes 262176 | tf_op jit(solution)/shard_map/ppermute | solution.py:295
  128.4 1.3 copy-done
  129.7 0.7 constant_dynamic-update-slice_fusion
  (42 shorter events, 0.5 us)
Async XLA Ops:
  1.9 17.2 %collective-permute-start = (bf16[128,640]{1,0:T(8,128)(2,1)S(1)}, bf16[128,640]{1,0:T(8,128)(2,1)S(1)}, u32[]{:S(2)}, u32[]{:S(2)}) collective-permute-start(bf16[128,640]{1,0:T(8,128)(2,1)S(1)} %maximum_maximum_fusion.refs_0_), channel_id=1, source_target_pairs={{0,2},{2,4},{4,6},{6,0},{1,3},{3,5},{5,7},{7,1},{8,10},{10,12},{12... | collective-permute-start | bytes 491528 | tf_op jit(solution)/shard_map/ppermute | solution.py:42
  3.1 15.9 %collective-permute-start.1 = (bf16[128,640]{1,0:T(8,128)(2,1)S(1)}, bf16[128,640]{1,0:T(8,128)(2,1)S(1)}, u32[]{:S(2)}, u32[]{:S(2)}) collective-permute-start(bf16[128,640]{1,0:T(8,128)(2,1)S(1)} %maximum_maximum_fusion.refs_0_), channel_id=1, source_target_pairs={{0,4},{2,6},{4,0},{6,2},{1,5},{3,7},{5,1},{7,3},{8,12},{10,14},{12... | collective-permute-start | bytes 491528 | tf_op jit(solution)/shard_map/ppermute | solution.py:42
  5.6 13.5 %collective-permute-start.2 = (bf16[128,640]{1,0:T(8,128)(2,1)S(1)}, bf16[128,640]{1,0:T(8,128)(2,1)S(1)}, u32[]{:S(2)}, u32[]{:S(2)}) collective-permute-start(bf16[128,640]{1,0:T(8,128)(2,1)S(1)} %maximum_maximum_fusion.refs_0_), channel_id=1, source_target_pairs={{0,6},{2,0},{4,2},{6,4},{1,7},{3,1},{5,3},{7,5},{8,14},{10,8},{12,... | collective-permute-start | bytes 491528 | tf_op jit(solution)/shard_map/ppermute | solution.py:42
  8.4 10.7 %copy-start.1 = (bf16[128,512]{1,0:T(8,128)(2,1)S(1)}, bf16[128,512]{1,0:T(8,128)(2,1)}, u32[]{:S(2)}) copy-start(bf16[128,512]{1,0:T(8,128)(2,1)} %param.7) | copy-start | bytes 393220
  8.4 27.9 %all-to-all-start = ((bf16[8,16,2048]{2,1,0:T(8,128)(2,1)}), bf16[8,16,2048]{2,1,0:T(8,128)(2,1)S(1)}, u32[]{:S(2)}, u32[]{:S(2)}) async-start(bf16[8,16,2048]{2,1,0:T(8,128)(2,1)} %broadcast_in_dim.43), calls=%async_computation | async-start | bytes 1048576 | tf_op jit(solution)/shard_map/all_to_all | solution.py:32
  16.5 19.2 %copy-start.4 = (s32[128]{0:T(128)S(1)}, s32[128]{0:T(128)}, u32[]{:S(2)}) copy-start(s32[128]{0:T(128)} %param.11) | copy-start | bytes 1540
  19.1 49.4 %collective-permute-start.16 = (bf16[128,1536]{1,0:T(8,128)(2,1)}, bf16[128,1536]{1,0:T(8,128)(2,1)}, u32[]{:S(2)}, u32[]{:S(2)}) collective-permute-start(bf16[128,1536]{1,0:T(8,128)(2,1)} %get-tuple-element.34), channel_id=1, source_target_pairs={{0,6},{1,7},{2,0},{3,1},{4,2},{5,3},{6,4},{7,5},{8,14},{9,15},{10,... | collective-permute-start | bytes 1179656 | tf_op jit(solution)/shard_map/ppermute | solution.py:272
  19.2 13.3 %collective-permute-start.5 = (bf16[128,640]{1,0:T(8,128)(2,1)S(1)}, bf16[128,640]{1,0:T(8,128)(2,1)S(1)}, u32[]{:S(2)}, u32[]{:S(2)}) collective-permute-start(bf16[128,640]{1,0:T(8,128)(2,1)S(1)} %select_select_fusion), channel_id=1, source_target_pairs={{0,8},{8,16},{16,24},{24,32},{32,40},{40,48},{48,56},{56,64},{64,7... | collective-permute-start | bytes 491528 | tf_op jit(solution)/shard_map/ppermute | solution.py:37
  32.6 6.9 %collective-permute-start.6 = (bf16[640,640]{1,0:T(8,128)(2,1)S(1)}, bf16[640,640]{1,0:T(8,128)(2,1)S(1)}, u32[]{:S(2)}, u32[]{:S(2)}) collective-permute-start(bf16[640,640]{1,0:T(8,128)(2,1)S(1)} %joined.1.mine_ref), channel_id=1, source_target_pairs={{0,1},{1,0},{2,3},{3,2},{4,5},{5,4},{6,7},{7,6},{8,9},{9,8},{10,11... | collective-permute-start | bytes 2457608 | tf_op jit(solution)/shard_map/ppermute | solution.py:46
  36.3 26.0 %collective-permute-start.7 = (bf16[128,2048]{1,0:T(8,128)(2,1)S(1)}, bf16[128,2048]{1,0:T(8,128)(2,1)S(1)}, u32[]{:S(2)}, u32[]{:S(2)}) collective-permute-start(bf16[128,2048]{1,0:T(8,128)(2,1)S(1)} %bitcast.11), channel_id=1, source_target_pairs={{0,8},{8,16},{16,24},{24,0},{1,9},{9,17},{17,25},{25,1},{2,10},{10... | collective-permute-start | bytes 1572872 | tf_op jit(solution)/shard_map/ppermute | solution.py:42
  36.3 26.2 %collective-permute-start.8 = (bf16[128,2048]{1,0:T(8,128)(2,1)S(1)}, bf16[128,2048]{1,0:T(8,128)(2,1)}, u32[]{:S(2)}, u32[]{:S(2)}) collective-permute-start(bf16[128,2048]{1,0:T(8,128)(2,1)S(1)} %bitcast.12), channel_id=1, source_target_pairs={{0,16},{8,24},{16,0},{24,8},{1,17},{9,25},{17,1},{25,9},{2,18},{10... | collective-permute-start | bytes 1572872 | tf_op jit(solution)/shard_map/ppermute | solution.py:42
  36.6 26.8 %collective-permute-start.9 = (bf16[128,2048]{1,0:T(8,128)(2,1)S(1)}, bf16[128,2048]{1,0:T(8,128)(2,1)}, u32[]{:S(2)}, u32[]{:S(2)}) collective-permute-start(bf16[128,2048]{1,0:T(8,128)(2,1)S(1)} %bitcast.13), channel_id=1, source_target_pairs={{0,24},{8,0},{16,8},{24,16},{1,25},{9,1},{17,9},{25,17},{2,26},{10... | collective-permute-start | bytes 1572872 | tf_op jit(solution)/shard_map/ppermute | solution.py:42
  39.4 22.8 %copy-start.3 = (bf16[128,1536]{1,0:T(8,128)(2,1)S(1)}, bf16[128,1536]{1,0:T(8,128)(2,1)}, u32[]{:S(2)}) copy-start(bf16[128,1536]{1,0:T(8,128)(2,1)} %get-tuple-element.33) | copy-start | bytes 1179652
  39.4 23.1 %copy-start.2 = (bf16[128,1536]{1,0:T(8,128)(2,1)S(1)}, bf16[128,1536]{1,0:T(8,128)(2,1)}, u32[]{:S(2)}) copy-start(bf16[128,1536]{1,0:T(8,128)(2,1)} %get-tuple-element.32) | copy-start | bytes 1179652
  39.6 32.2 %collective-permute-start.17 = (bf16[128,1536]{1,0:T(8,128)(2,1)}, bf16[128,1536]{1,0:T(8,128)(2,1)S(1)}, u32[]{:S(2)}, u32[]{:S(2)}) collective-permute-start(bf16[128,1536]{1,0:T(8,128)(2,1)} %get-tuple-element.31), channel_id=1, source_target_pairs={{0,7},{1,6},{2,1},{3,0},{4,3},{5,2},{6,5},{7,4},{8,15},{9,14},{10,... | collective-permute-start | bytes 1179656 | tf_op jit(solution)/shard_map/ppermute | solution.py:272
  62.2 13.6 %collective-permute-start.12 = (bf16[128,1536]{1,0:T(8,128)(2,1)S(1)}, bf16[128,1536]{1,0:T(8,128)(2,1)S(1)}, u32[]{:S(2)}, u32[]{:S(2)}) collective-permute-start(bf16[128,1536]{1,0:T(8,128)(2,1)S(1)} %copy-done.3), channel_id=1, source_target_pairs={{0,2},{1,3},{2,4},{3,5},{4,6},{5,7},{6,0},{7,1},{8,10},{9,11},{10,... | collective-permute-start | bytes 1179656 | tf_op jit(solution)/shard_map/ppermute | solution.py:272
  62.6 38.3 %collective-permute-start.13 = (bf16[128,1536]{1,0:T(8,128)(2,1)S(1)}, bf16[128,1536]{1,0:T(8,128)(2,1)S(1)}, u32[]{:S(2)}, u32[]{:S(2)}) collective-permute-start(bf16[128,1536]{1,0:T(8,128)(2,1)S(1)} %copy-done.2), channel_id=1, source_target_pairs={{0,3},{1,2},{2,5},{3,4},{4,7},{5,6},{6,1},{7,0},{8,11},{9,10},{10,... | collective-permute-start | bytes 1179656 | tf_op jit(solution)/shard_map/ppermute | solution.py:272
  63.4 47.1 %collective-permute-start.20 = (bf16[128,1536]{1,0:T(8,128)(2,1)S(1)}, bf16[128,1536]{1,0:T(8,128)(2,1)S(1)}, u32[]{:S(2)}, u32[]{:S(2)}) collective-permute-start(bf16[128,1536]{1,0:T(8,128)(2,1)S(1)} %get-tuple-element.27), channel_id=1, source_target_pairs={{0,1},{1,0},{2,3},{3,2},{4,5},{5,4},{6,7},{7,6},{8,9},{9,8},{10,11... | collective-permute-start | bytes 1179656 | tf_op jit(solution)/shard_map/ppermute | solution.py:272
  68.5 35.6 %collective-permute-start.3 = (bf16[128,1536]{1,0:T(8,128)(2,1)S(1)}, bf16[128,1536]{1,0:T(8,128)(2,1)S(1)}, u32[]{:S(2)}, u32[]{:S(2)}) collective-permute-start(bf16[128,1536]{1,0:T(8,128)(2,1)S(1)} %get-tuple-element.30), channel_id=1, source_target_pairs={{0,4},{1,5},{2,6},{3,7},{4,0},{5,1},{6,2},{7,3},{8,12},{9,13},{10,... | collective-permute-start | bytes 1179656 | tf_op jit(solution)/shard_map/ppermute | solution.py:272
  71.8 32.3 %collective-permute-start.4 = (bf16[128,1536]{1,0:T(8,128)(2,1)S(1)}, bf16[128,1536]{1,0:T(8,128)(2,1)S(1)}, u32[]{:S(2)}, u32[]{:S(2)}) collective-permute-start(bf16[128,1536]{1,0:T(8,128)(2,1)S(1)} %get-tuple-element.29), channel_id=1, source_target_pairs={{0,5},{1,4},{2,7},{3,6},{4,1},{5,0},{6,3},{7,2},{8,13},{9,12},{10,... | collective-permute-start | bytes 1179656 | tf_op jit(solution)/shard_map/ppermute | solution.py:272
  75.9 50.9 %collective-permute-start.18 = (bf16[128,1024]{1,0:T(8,128)(2,1)S(1)}, bf16[128,1024]{1,0:T(8,128)(2,1)S(1)}, u32[]{:S(2)}, u32[]{:S(2)}) collective-permute-start(bf16[128,1024]{1,0:T(8,128)(2,1)S(1)} %get-tuple-element.23), channel_id=1, source_target_pairs={{6,0},{7,1},{0,2},{1,3},{2,4},{3,5},{4,6},{5,7},{14,8},{15,9},{8,1... | collective-permute-start | bytes 786440 | tf_op jit(solution)/shard_map/ppermute | solution.py:295
  104.0 19.1 %collective-permute-start.14 = (bf16[128,1024]{1,0:T(8,128)(2,1)S(1)}, bf16[128,1024]{1,0:T(8,128)(2,1)S(1)}, u32[]{:S(2)}, u32[]{:S(2)}) collective-permute-start(bf16[128,1024]{1,0:T(8,128)(2,1)S(1)} %get-tuple-element.21), channel_id=1, source_target_pairs={{2,0},{3,1},{4,2},{5,3},{6,4},{7,5},{0,6},{1,7},{10,8},{11,9},{12,... | collective-permute-start | bytes 786440 | tf_op jit(solution)/shard_map/ppermute | solution.py:295
  107.2 9.4 %collective-permute-start.10 = (bf16[128,1024]{1,0:T(8,128)(2,1)S(1)}, bf16[128,1024]{1,0:T(8,128)(2,1)S(1)}, u32[]{:S(2)}, u32[]{:S(2)}) collective-permute-start(bf16[128,1024]{1,0:T(8,128)(2,1)S(1)} %get-tuple-element.19), channel_id=1, source_target_pairs={{4,0},{5,1},{6,2},{7,3},{0,4},{1,5},{2,6},{3,7},{12,8},{13,9},{14,... | collective-permute-start | bytes 786440 | tf_op jit(solution)/shard_map/ppermute | solution.py:295
  107.3 15.7 %collective-permute-start.11 = (bf16[128,1024]{1,0:T(8,128)(2,1)S(1)}, bf16[128,1024]{1,0:T(8,128)(2,1)S(1)}, u32[]{:S(2)}, u32[]{:S(2)}) collective-permute-start(bf16[128,1024]{1,0:T(8,128)(2,1)S(1)} %get-tuple-element.20), channel_id=1, source_target_pairs={{5,0},{4,1},{7,2},{6,3},{1,4},{0,5},{3,6},{2,7},{13,8},{12,9},{15,... | collective-permute-start | bytes 786440 | tf_op jit(solution)/shard_map/ppermute | solution.py:295
  110.6 16.2 %collective-permute-start.15 = (bf16[128,1024]{1,0:T(8,128)(2,1)S(1)}, bf16[128,1024]{1,0:T(8,128)(2,1)S(1)}, u32[]{:S(2)}, u32[]{:S(2)}) collective-permute-start(bf16[128,1024]{1,0:T(8,128)(2,1)S(1)} %get-tuple-element.22), channel_id=1, source_target_pairs={{3,0},{2,1},{5,2},{4,3},{7,4},{6,5},{1,6},{0,7},{11,8},{10,9},{13,... | collective-permute-start | bytes 786440 | tf_op jit(solution)/shard_map/ppermute | solution.py:295
  116.6 11.7 %collective-permute-start.19 = (bf16[128,1024]{1,0:T(8,128)(2,1)S(1)}, bf16[128,1024]{1,0:T(8,128)(2,1)S(1)}, u32[]{:S(2)}, u32[]{:S(2)}) collective-permute-start(bf16[128,1024]{1,0:T(8,128)(2,1)S(1)} %get-tuple-element.24), channel_id=1, source_target_pairs={{7,0},{6,1},{1,2},{0,3},{3,4},{2,5},{5,6},{4,7},{15,8},{14,9},{9,1... | collective-permute-start | bytes 786440 | tf_op jit(solution)/shard_map/ppermute | solution.py:295
  123.0 5.4 %collective-permute-start.21 = (bf16[128,1024]{1,0:T(8,128)(2,1)S(1)}, bf16[128,1024]{1,0:T(8,128)(2,1)S(1)}, u32[]{:S(2)}, u32[]{:S(2)}) collective-permute-start(bf16[128,1024]{1,0:T(8,128)(2,1)S(1)} %get-tuple-element.26), channel_id=1, source_target_pairs={{1,0},{0,1},{3,2},{2,3},{5,4},{4,5},{7,6},{6,7},{9,8},{8,9},{11,10... | collective-permute-start | bytes 786440 | tf_op jit(solution)/shard_map/ppermute | solution.py:295
  128.4 1.3 %copy-start = (bf16[128,8192]{1,0:T(8,128)(2,1)}, bf16[128,8192]{1,0:T(8,128)(2,1)S(1)}, u32[]{:S(2)}) copy-start(bf16[128,8192]{1,0:T(8,128)(2,1)S(1)} %constant_dynamic-update-slice_fusion.1) | copy-start | bytes 6291460

commit v3 on v2

--- a/solution.py
+++ b/solution.py
@@ -20,6 +20,7 @@
 GROUP = ("x", "c")
 EVERY = ("z", "y", "x", "c")
 CHUNK = 640
+TOGETHER = 8
 STRIP = 16
 VMEM_LIMIT = 24 * 2**20
 INTERPRET = False
@@ -172,20 +173,20 @@
         bias_ref[at : at + STRIP, :] = jnp.where(allowed, 0.0, LOWEST)
     span = pl.ds(base, window)
 
-    @pl.loop(0, heads // 2)
-    def _(pair):
-        for half in range(2):
-            q_at = pl.multiple_of(pair * 2 * (NOPE + ROPE) + 128 * half, 128)
-            v_at = pl.ds(pl.multiple_of((2 * pair + half) * VDIM, VDIM), VDIM)
-            k_at = pl.ds(pl.multiple_of((2 * pair + half) * WIDE, WIDE), WIDE)
+    @pl.loop(0, heads // TOGETHER)
+    def _(turn):
+        for half in range(TOGETHER):
+            q_at = (turn * TOGETHER + half // 2 * 2) * (NOPE + ROPE) + 128 * (half % 2)
+            q_at = pl.multiple_of(q_at, 128)
+            k_at = pl.ds(pl.multiple_of((TOGETHER * turn + half) * WIDE, WIDE), WIDE)
             s_ref[half] = lax.dot_general(
                 q_ref[:, pl.ds(q_at, WIDE)],
                 k_ref[span, k_at],
                 (((1,), (1,)), ((), ())),
                 preferred_element_type=jnp.float32,
             )
-        for half in range(2):
-            v_at = pl.ds(pl.multiple_of((2 * pair + half) * VDIM, VDIM), VDIM)
+        for half in range(TOGETHER):
+            v_at = pl.ds(pl.multiple_of((TOGETHER * turn + half) * VDIM, VDIM), VDIM)
             for at in range(0, rows, STRIP):
                 part = slice(at, at + STRIP)
                 scores = s_ref[half, part, :] * score_scale + bias_ref[part, :]
@@ -218,9 +219,9 @@
             pltpu.VMEM((2 * SUB, width), jnp.bfloat16),
             pltpu.VMEM((2 * SUB, heads * VDIM), jnp.bfloat16),
             pltpu.VMEM((2 * SUB, window), jnp.float32),
-            pltpu.VMEM((2, 2 * SUB, window), jnp.float32),
-            pltpu.VMEM((2, 2 * SUB, window), jnp.bfloat16),
-            pltpu.VMEM((2, 2 * SUB, VDIM), jnp.float32),
+            pltpu.VMEM((TOGETHER, 2 * SUB, window), jnp.float32),
+            pltpu.VMEM((TOGETHER, 2 * SUB, window), jnp.bfloat16),
+            pltpu.VMEM((TOGETHER, 2 * SUB, VDIM), jnp.float32),
         ],
         compiler_params=pltpu.CompilerParams(vmem_limit_bytes=VMEM_LIMIT),
         cost_estimate=pl.CostEstimate(

time: 131 us -> 130 us (level)
  Pallas kernels: 17.5 us -> 16 us
    pallas_call x4, Pallas kernels: 12.9 us -> 11.4 us  [attend(): pl.pallas_call(functools.partial(attend_kernel, score_scale), in_specs=[I...]
  transfers between devices with their start and end apart: 23 -> 23, of which waited for: 7 -> 7; matrix products, arithmetic and copies ran while one was open for 6% -> 6% of each run, Pallas kernels for 13% -> 12%
where the time goes in v3:
time: 130 us
  waiting for transfers between devices  69.2 us (53%)
  starting transfers between devices  33 us (25%)
  Pallas kernels  16 us (12%)
  local copies, waits for them, and re-layouts  8.4 us (6%)
  other arithmetic  2.7 us (2%)
    ppermute x7, waiting for transfers between devices, sent(): return lax.ppermute(out, GROUP, hops(step, flip))  25.1 us
    ppermute x6, waiting for transfers between devices, turned(): lax.ppermute(value, axis, [(i, (i + steps) % count) for i in range(count)])  20.6 us
    ppermute x7, waiting for transfers between devices, whole(): back = lax.ppermute(back, GROUP, [(b, a) for a, b in hops(step, flip)])  13.4 us
    pallas_call x4, Pallas kernels, attend(): pl.pallas_call(functools.partial(attend_kernel, score_scale), in_specs=[I...  11.4 us
    ppermute x1, waiting for transfers between devices, shifted(): lax.ppermute(value, axes, [(i, i + steps) for i in range(count - steps)])  10 us
    all_to_all x1, starting transfers between devices, spread(): return lax.all_to_all(copies, axis, 0, 0)  8.14 us
    ppermute x6, starting transfers between devices, turned(): lax.ppermute(value, axis, [(i, (i + steps) % count) for i in range(count)])  7.64 us
    ppermute x7, starting transfers between devices, sent(): return lax.ppermute(out, GROUP, hops(step, flip))  6.09 us
  transfers between devices with their start and end apart: 23, of which 7 were waited for; matrix products, arithmetic and copies ran while one was open for 6% of the time, Pallas kernels for 12%

profile of v3, /device:TPU:33, one launch (start us, length us, event | category | flops | bytes accessed | tf_op | source)
XLA Modules:
  0.0 129.7 jit_solution(4279698140953660628)
XLA Ops:
  0.0 0.8 copy.13
  0.8 0.1 pad.16.clone
  0.9 0.9 maximum_maximum_fusion.refs_0_
  1.9 1.3 collective-permute-start
  3.1 2.5 %collective-permute-start.1 = (bf16[128,640]{1,0:T(8,128)(2,1)S(1)}, bf16[128,640]{1,0:T(8,128)(2,1)S(1)}, u32[]{:S(2)}, u32[]{:S(2)}) collective-permute-start(bf16[128,640]{1,0:T(8,128)(2,1)S(1)} %maximum_maximum_fusion.refs_0_), channel_id=1, source_target_pairs={{0,4},{2,6},{4,0},{6,2},{1,5},{3,7},{5,1},{7,3},{8,12},{10,14},{12... | collective-permute-start | bytes 491528 | tf_op jit(solution)/shard_map/ppermute | solution.py:43
  5.6 1.2 collective-permute-start.2
  6.8 0.8 pad_maximum_fusion
  7.5 0.8 broadcast_in_dim.43
  8.4 8.1 %all-to-all-start = ((bf16[8,16,2048]{2,1,0:T(8,128)(2,1)}), bf16[8,16,2048]{2,1,0:T(8,128)(2,1)S(1)}, u32[]{:S(2)}, u32[]{:S(2)}) async-start(bf16[8,16,2048]{2,1,0:T(8,128)(2,1)} %broadcast_in_dim.43), calls=%async_computation | async-start | bytes 1048576 | tf_op jit(solution)/shard_map/all_to_all | solution.py:33
  16.5 2.6 %constant_dynamic-slice_fusion.2 = (bf16[128,1536]{1,0:T(8,128)(2,1)}, bf16[128,1536]{1,0:T(8,128)(2,1)}, bf16[128,1536]{1,0:T(8,128)(2,1)}, bf16[128,1536]{1,0:T(8,128)(2,1)}) fusion(bf16[128,12288]{1,0:T(8,128)(2,1)} %param.6, s32[]{:T(128)S(6)} %select_n.103, s32[]{:T(128)S(6)} %select_n.99, s32[]{:T(128)S(6)} %select_n.98, s32[]{:T(128)S(6)} %select_n.102), kind=kLoop, calls=%fused_computation.14 | loop fusion | bytes 3145744 | tf_op jit(solution)/shard_map/dynamic_slice | solution.py:270
  19.1 0.1 select_select_fusion
  19.2 3.2 %collective-permute-start.5 = (bf16[128,640]{1,0:T(8,128)(2,1)S(1)}, bf16[128,640]{1,0:T(8,128)(2,1)S(1)}, u32[]{:S(2)}, u32[]{:S(2)}) collective-permute-start(bf16[128,640]{1,0:T(8,128)(2,1)S(1)} %select_select_fusion), channel_id=1, source_target_pairs={{0,8},{8,16},{16,24},{24,32},{32,40},{40,48},{48,56},{56,64},{64,7... | collective-permute-start | bytes 491528 | tf_op jit(solution)/shard_map/ppermute | solution.py:38
  22.4 0.1 add_add_fusion.3.at_ref
  22.5 10.0 %collective-permute-done.5.refs_4_ = bf16[128,640]{1,0:T(8,128)(2,1)S(1)} collective-permute-done((bf16[128,640]{1,0:T(8,128)(2,1)S(1)}, bf16[128,640]{1,0:T(8,128)(2,1)S(1)}, u32[]{:S(2)}, u32[]{:S(2)}) %collective-permute-start.5) | collective-permute-done | bytes 163872 | tf_op jit(solution)/shard_map/ppermute | solution.py:38
  32.6 3.0 %collective-permute-start.6 = (bf16[640,640]{1,0:T(8,128)(2,1)S(1)}, bf16[640,640]{1,0:T(8,128)(2,1)S(1)}, u32[]{:S(2)}, u32[]{:S(2)}) collective-permute-start(bf16[640,640]{1,0:T(8,128)(2,1)S(1)} %joined.1.mine_ref), channel_id=1, source_target_pairs={{0,1},{1,0},{2,3},{3,2},{4,5},{5,4},{6,7},{7,6},{8,9},{9,8},{10,11... | collective-permute-start | bytes 2457608 | tf_op jit(solution)/shard_map/ppermute | solution.py:47
  35.7 0.1 select_reduce_fusion.1
  35.9 0.4 select_reduce_fusion
  36.3 0.1 collective-permute-start.7
  36.3 0.3 collective-permute-start.8
  36.6 2.4 %collective-permute-start.9 = (bf16[128,2048]{1,0:T(8,128)(2,1)S(1)}, bf16[128,2048]{1,0:T(8,128)(2,1)}, u32[]{:S(2)}, u32[]{:S(2)}) collective-permute-start(bf16[128,2048]{1,0:T(8,128)(2,1)S(1)} %bitcast.13), channel_id=1, source_target_pairs={{0,24},{8,0},{16,8},{24,16},{1,25},{9,1},{17,9},{25,17},{2,26},{10... | collective-permute-start | bytes 1572872 | tf_op jit(solution)/shard_map/ppermute | solution.py:43
  39.1 0.2 copy.14.start_ref
  39.4 0.1 add_add_fusion.at_ref
  39.6 0.6 collective-permute-start.17
  40.2 1.5 %constant_dynamic-slice_fusion = (bf16[128,1536]{1,0:T(8,128)(2,1)S(1)}, bf16[128,1536]{1,0:T(8,128)(2,1)S(1)}, bf16[128,1536]{1,0:T(8,128)(2,1)S(1)}, bf16[128,1536]{1,0:T(8,128)(2,1)S(1)}) fusion(bf16[128,12288]{1,0:T(8,128)(2,1)} %param.6, s32[]{:T(128)S(6)} %select_n.107, s32[]{:T(128)S(6)} %select_n.106, s32[]{:T(128)S(6)} %select_n.93, s32[]{:T(128)S(6)} %select_n.92), kind=kLoop, calls=%fused_computation.10 | loop fusion | bytes 3145744 | tf_op jit(solution)/shard_map/dynamic_slice | solution.py:270
  41.7 20.6 %collective-permute-done.7.refs_1_ = bf16[128,2048]{1,0:T(8,128)(2,1)S(1)} collective-permute-done((bf16[128,2048]{1,0:T(8,128)(2,1)S(1)}, bf16[128,2048]{1,0:T(8,128)(2,1)S(1)}, u32[]{:S(2)}, u32[]{:S(2)}) %collective-permute-start.7) | collective-permute-done | bytes 524320 | tf_op jit(solution)/shard_map/ppermute | solution.py:43
  62.2 0.3 collective-permute-start.12
  62.6 0.9 collective-permute-start.13
  63.4 0.6 collective-permute-start.20
  64.0 4.5 %project.1 = (bf16[1280,2048]{1,0:T(8,128)(2,1)S(1)}, bf16[1280,1024]{1,0:T(8,128)(2,1)S(1)}) custom-call(s32[3]{0:T(128)S(1)} %pad_add_fusion.at_ref, bf16[640,640]{1,0:T(8,128)(2,1)S(1)} %joined.1.mine_ref, bf16[640,640]{1,0:T(8,128)(2,1)S(1)} %collective-permute-done.6.other_ref, bf16[128,2048]{1,0:T(8,128)(2,1)S(1)} %bitcast.14, ...), custom_call_target="tpu_custom_call" | custom-call | flops 2684354560 | bytes 10485760 | tf_op jit(solution)/shard_map/project/pallas_call | solution.py:137
  68.5 3.2 %collective-permute-start.3 = (bf16[128,1536]{1,0:T(8,128)(2,1)S(1)}, bf16[128,1536]{1,0:T(8,128)(2,1)S(1)}, u32[]{:S(2)}, u32[]{:S(2)}) collective-permute-start(bf16[128,1536]{1,0:T(8,128)(2,1)S(1)} %get-tuple-element.30), channel_id=1, source_target_pairs={{0,4},{1,5},{2,6},{3,7},{4,0},{5,1},{6,2},{7,3},{8,12},{9,13},{10,... | collective-permute-start | bytes 1179656 | tf_op jit(solution)/shard_map/ppermute | solution.py:273
  71.8 0.5 collective-permute-start.4
  72.3 3.2 %attend.6 = (bf16[128,1024]{1,0:T(8,128)(2,1)S(1)}, bf16[128,1024]{1,0:T(8,128)(2,1)S(1)}) custom-call(s32[3]{0:T(128)S(1)} %add_add_fusion.2.at_ref, bf16[128,1536]{1,0:T(8,128)(2,1)} %collective-permute-done.16.q0_ref, bf16[128,1536]{1,0:T(8,128)(2,1)S(1)} %collective-permute-done.17.q1_ref, bf16[1280,2048]{1,0:T(8,128)(2,1)S(1)} %get-tuple-element.17.k_ref, ...), custom_call_target="tpu_custom_call" | custom-call | flops 8053063680 | bytes 4194304 | tf_op jit(solution)/shard_map/attend/pallas_call | solution.py:213
  75.5 0.3 collective-permute-start.18
  75.8 25.1 %collective-permute-done.13.q1_ref = bf16[128,1536]{1,0:T(8,128)(2,1)S(1)} collective-permute-done((bf16[128,1536]{1,0:T(8,128)(2,1)S(1)}, bf16[128,1536]{1,0:T(8,128)(2,1)S(1)}, u32[]{:S(2)}, u32[]{:S(2)}) %collective-permute-start.13) | collective-permute-done | bytes 393248 | tf_op jit(solution)/shard_map/ppermute | solution.py:273
  100.9 2.7 %attend.5 = (bf16[128,1024]{1,0:T(8,128)(2,1)S(1)}, bf16[128,1024]{1,0:T(8,128)(2,1)S(1)}) custom-call(s32[3]{0:T(128)S(1)} %add_add_fusion.1.at_ref, bf16[128,1536]{1,0:T(8,128)(2,1)S(1)} %collective-permute-done.12.q0_ref, bf16[128,1536]{1,0:T(8,128)(2,1)S(1)} %collective-permute-done.13.q1_ref, bf16[1280,2048]{1,0:T(8,128)(2,1)S(1)} %get-tuple-element.17.k_ref, ...), custom_call_target="tpu_custom_call" | custom-call | flops 8053063680 | bytes 4194304 | tf_op jit(solution)/shard_map/attend/pallas_call | solution.py:213
  103.6 0.1 collective-permute-start.14
  103.7 2.7 %attend.4 = (bf16[128,1024]{1,0:T(8,128)(2,1)S(1)}, bf16[128,1024]{1,0:T(8,128)(2,1)S(1)}) custom-call(s32[3]{0:T(128)S(1)} %add_add_fusion.at_ref, bf16[128,1536]{1,0:T(8,128)(2,1)S(1)} %collective-permute-done.3.q0_ref, bf16[128,1536]{1,0:T(8,128)(2,1)S(1)} %collective-permute-done.4.q1_ref, bf16[1280,2048]{1,0:T(8,128)(2,1)S(1)} %get-tuple-element.17.k_ref, ...), custom_call_target="tpu_custom_call" | custom-call | flops 8053063680 | bytes 4194304 | tf_op jit(solution)/shard_map/attend/pallas_call | solution.py:213
  106.5 0.1 collective-permute-start.10
  106.6 3.2 %collective-permute-start.11 = (bf16[128,1024]{1,0:T(8,128)(2,1)S(1)}, bf16[128,1024]{1,0:T(8,128)(2,1)S(1)}, u32[]{:S(2)}, u32[]{:S(2)}) collective-permute-start(bf16[128,1024]{1,0:T(8,128)(2,1)S(1)} %get-tuple-element.20), channel_id=1, source_target_pairs={{5,0},{4,1},{7,2},{6,3},{1,4},{0,5},{3,6},{2,7},{13,8},{12,9},{15,... | collective-permute-start | bytes 786440 | tf_op jit(solution)/shard_map/ppermute | solution.py:296
  109.8 1.2 collective-permute-start.15
  111.0 2.7 %attend.7 = (bf16[128,1024]{1,0:T(8,128)(2,1)S(1)}, bf16[128,1024]{1,0:T(8,128)(2,1)S(1)}) custom-call(s32[3]{0:T(128)S(1)} %add_add_fusion.3.at_ref, bf16[128,1536]{1,0:T(8,128)(2,1)S(1)} %get-tuple-element.28.q0_ref, bf16[128,1536]{1,0:T(8,128)(2,1)S(1)} %collective-permute-done.20.q1_ref, bf16[1280,2048]{1,0:T(8,128)(2,1)S(1)} %get-tuple-element.17.k_ref, ...), custom_call_target="tpu_custom_call" | custom-call | flops 8053063680 | bytes 4194304 | tf_op jit(solution)/shard_map/attend/pallas_call | solution.py:213
  113.8 2.1 %collective-permute-done.10 = bf16[128,1024]{1,0:T(8,128)(2,1)S(1)} collective-permute-done((bf16[128,1024]{1,0:T(8,128)(2,1)S(1)}, bf16[128,1024]{1,0:T(8,128)(2,1)S(1)}, u32[]{:S(2)}, u32[]{:S(2)}) %collective-permute-start.10) | collective-permute-done | bytes 262176 | tf_op jit(solution)/shard_map/ppermute | solution.py:296
  115.9 0.2 broadcast_in_dim.28
  116.1 6.1 %collective-permute-done.11 = bf16[128,1024]{1,0:T(8,128)(2,1)S(1)} collective-permute-done((bf16[128,1024]{1,0:T(8,128)(2,1)S(1)}, bf16[128,1024]{1,0:T(8,128)(2,1)S(1)}, u32[]{:S(2)}, u32[]{:S(2)}) %collective-permute-start.11) | collective-permute-done | bytes 262176 | tf_op jit(solution)/shard_map/ppermute | solution.py:296
  122.3 4.1 %collective-permute-done.15 = bf16[128,1024]{1,0:T(8,128)(2,1)S(1)} collective-permute-done((bf16[128,1024]{1,0:T(8,128)(2,1)S(1)}, bf16[128,1024]{1,0:T(8,128)(2,1)S(1)}, u32[]{:S(2)}, u32[]{:S(2)}) %collective-permute-start.15) | collective-permute-done | bytes 262176 | tf_op jit(solution)/shard_map/ppermute | solution.py:296
  126.5 1.1 collective-permute-done.19
  127.7 1.3 %copy-done = bf16[128,8192]{1,0:T(8,128)(2,1)} copy-done((bf16[128,8192]{1,0:T(8,128)(2,1)}, bf16[128,8192]{1,0:T(8,128)(2,1)S(1)}, u32[]{:S(2)}) %copy-start) | copy-done | bytes 2097176
  129.0 0.7 constant_dynamic-update-slice_fusion
  (42 shorter events, 0.5 us)
Async XLA Ops:
  1.9 17.2 %collective-permute-start = (bf16[128,640]{1,0:T(8,128)(2,1)S(1)}, bf16[128,640]{1,0:T(8,128)(2,1)S(1)}, u32[]{:S(2)}, u32[]{:S(2)}) collective-permute-start(bf16[128,640]{1,0:T(8,128)(2,1)S(1)} %maximum_maximum_fusion.refs_0_), channel_id=1, source_target_pairs={{0,2},{2,4},{4,6},{6,0},{1,3},{3,5},{5,7},{7,1},{8,10},{10,12},{12... | collective-permute-start | bytes 491528 | tf_op jit(solution)/shard_map/ppermute | solution.py:43
  3.1 15.9 %collective-permute-start.1 = (bf16[128,640]{1,0:T(8,128)(2,1)S(1)}, bf16[128,640]{1,0:T(8,128)(2,1)S(1)}, u32[]{:S(2)}, u32[]{:S(2)}) collective-permute-start(bf16[128,640]{1,0:T(8,128)(2,1)S(1)} %maximum_maximum_fusion.refs_0_), channel_id=1, source_target_pairs={{0,4},{2,6},{4,0},{6,2},{1,5},{3,7},{5,1},{7,3},{8,12},{10,14},{12... | collective-permute-start | bytes 491528 | tf_op jit(solution)/shard_map/ppermute | solution.py:43
  5.6 13.5 %collective-permute-start.2 = (bf16[128,640]{1,0:T(8,128)(2,1)S(1)}, bf16[128,640]{1,0:T(8,128)(2,1)S(1)}, u32[]{:S(2)}, u32[]{:S(2)}) collective-permute-start(bf16[128,640]{1,0:T(8,128)(2,1)S(1)} %maximum_maximum_fusion.refs_0_), channel_id=1, source_target_pairs={{0,6},{2,0},{4,2},{6,4},{1,7},{3,1},{5,3},{7,5},{8,14},{10,8},{12,... | collective-permute-start | bytes 491528 | tf_op jit(solution)/shard_map/ppermute | solution.py:43
  8.4 10.7 %copy-start.1 = (bf16[128,512]{1,0:T(8,128)(2,1)S(1)}, bf16[128,512]{1,0:T(8,128)(2,1)}, u32[]{:S(2)}) copy-start(bf16[128,512]{1,0:T(8,128)(2,1)} %param.7) | copy-start | bytes 393220
  8.4 27.9 %all-to-all-start = ((bf16[8,16,2048]{2,1,0:T(8,128)(2,1)}), bf16[8,16,2048]{2,1,0:T(8,128)(2,1)S(1)}, u32[]{:S(2)}, u32[]{:S(2)}) async-start(bf16[8,16,2048]{2,1,0:T(8,128)(2,1)} %broadcast_in_dim.43), calls=%async_computation | async-start | bytes 1048576 | tf_op jit(solution)/shard_map/all_to_all | solution.py:33
  16.5 19.2 %copy-start.4 = (s32[128]{0:T(128)S(1)}, s32[128]{0:T(128)}, u32[]{:S(2)}) copy-start(s32[128]{0:T(128)} %param.11) | copy-start | bytes 1540
  19.1 49.4 %collective-permute-start.16 = (bf16[128,1536]{1,0:T(8,128)(2,1)}, bf16[128,1536]{1,0:T(8,128)(2,1)}, u32[]{:S(2)}, u32[]{:S(2)}) collective-permute-start(bf16[128,1536]{1,0:T(8,128)(2,1)} %get-tuple-element.34), channel_id=1, source_target_pairs={{0,6},{1,7},{2,0},{3,1},{4,2},{5,3},{6,4},{7,5},{8,14},{9,15},{10,... | collective-permute-start | bytes 1179656 | tf_op jit(solution)/shard_map/ppermute | solution.py:273
  19.2 13.3 %collective-permute-start.5 = (bf16[128,640]{1,0:T(8,128)(2,1)S(1)}, bf16[128,640]{1,0:T(8,128)(2,1)S(1)}, u32[]{:S(2)}, u32[]{:S(2)}) collective-permute-start(bf16[128,640]{1,0:T(8,128)(2,1)S(1)} %select_select_fusion), channel_id=1, source_target_pairs={{0,8},{8,16},{16,24},{24,32},{32,40},{40,48},{48,56},{56,64},{64,7... | collective-permute-start | bytes 491528 | tf_op jit(solution)/shard_map/ppermute | solution.py:38
  32.6 6.9 %collective-permute-start.6 = (bf16[640,640]{1,0:T(8,128)(2,1)S(1)}, bf16[640,640]{1,0:T(8,128)(2,1)S(1)}, u32[]{:S(2)}, u32[]{:S(2)}) collective-permute-start(bf16[640,640]{1,0:T(8,128)(2,1)S(1)} %joined.1.mine_ref), channel_id=1, source_target_pairs={{0,1},{1,0},{2,3},{3,2},{4,5},{5,4},{6,7},{7,6},{8,9},{9,8},{10,11... | collective-permute-start | bytes 2457608 | tf_op jit(solution)/shard_map/ppermute | solution.py:47
  36.3 26.0 %collective-permute-start.7 = (bf16[128,2048]{1,0:T(8,128)(2,1)S(1)}, bf16[128,2048]{1,0:T(8,128)(2,1)S(1)}, u32[]{:S(2)}, u32[]{:S(2)}) collective-permute-start(bf16[128,2048]{1,0:T(8,128)(2,1)S(1)} %bitcast.11), channel_id=1, source_target_pairs={{0,8},{8,16},{16,24},{24,0},{1,9},{9,17},{17,25},{25,1},{2,10},{10... | collective-permute-start | bytes 1572872 | tf_op jit(solution)/shard_map/ppermute | solution.py:43
  36.3 26.2 %collective-permute-start.8 = (bf16[128,2048]{1,0:T(8,128)(2,1)S(1)}, bf16[128,2048]{1,0:T(8,128)(2,1)}, u32[]{:S(2)}, u32[]{:S(2)}) collective-permute-start(bf16[128,2048]{1,0:T(8,128)(2,1)S(1)} %bitcast.12), channel_id=1, source_target_pairs={{0,16},{8,24},{16,0},{24,8},{1,17},{9,25},{17,1},{25,9},{2,18},{10... | collective-permute-start | bytes 1572872 | tf_op jit(solution)/shard_map/ppermute | solution.py:43
  36.6 26.8 %collective-permute-start.9 = (bf16[128,2048]{1,0:T(8,128)(2,1)S(1)}, bf16[128,2048]{1,0:T(8,128)(2,1)}, u32[]{:S(2)}, u32[]{:S(2)}) collective-permute-start(bf16[128,2048]{1,0:T(8,128)(2,1)S(1)} %bitcast.13), channel_id=1, source_target_pairs={{0,24},{8,0},{16,8},{24,16},{1,25},{9,1},{17,9},{25,17},{2,26},{10... | collective-permute-start | bytes 1572872 | tf_op jit(solution)/shard_map/ppermute | solution.py:43
  39.4 22.8 %copy-start.3 = (bf16[128,1536]{1,0:T(8,128)(2,1)S(1)}, bf16[128,1536]{1,0:T(8,128)(2,1)}, u32[]{:S(2)}) copy-start(bf16[128,1536]{1,0:T(8,128)(2,1)} %get-tuple-element.33) | copy-start | bytes 1179652
  39.4 23.1 %copy-start.2 = (bf16[128,1536]{1,0:T(8,128)(2,1)S(1)}, bf16[128,1536]{1,0:T(8,128)(2,1)}, u32[]{:S(2)}) copy-start(bf16[128,1536]{1,0:T(8,128)(2,1)} %get-tuple-element.32) | copy-start | bytes 1179652
  39.6 32.2 %collective-permute-start.17 = (bf16[128,1536]{1,0:T(8,128)(2,1)}, bf16[128,1536]{1,0:T(8,128)(2,1)S(1)}, u32[]{:S(2)}, u32[]{:S(2)}) collective-permute-start(bf16[128,1536]{1,0:T(8,128)(2,1)} %get-tuple-element.31), channel_id=1, source_target_pairs={{0,7},{1,6},{2,1},{3,0},{4,3},{5,2},{6,5},{7,4},{8,15},{9,14},{10,... | collective-permute-start | bytes 1179656 | tf_op jit(solution)/shard_map/ppermute | solution.py:273
  62.2 13.3 %collective-permute-start.12 = (bf16[128,1536]{1,0:T(8,128)(2,1)S(1)}, bf16[128,1536]{1,0:T(8,128)(2,1)S(1)}, u32[]{:S(2)}, u32[]{:S(2)}) collective-permute-start(bf16[128,1536]{1,0:T(8,128)(2,1)S(1)} %copy-done.3), channel_id=1, source_target_pairs={{0,2},{1,3},{2,4},{3,5},{4,6},{5,7},{6,0},{7,1},{8,10},{9,11},{10,... | collective-permute-start | bytes 1179656 | tf_op jit(solution)/shard_map/ppermute | solution.py:273
  62.6 38.3 %collective-permute-start.13 = (bf16[128,1536]{1,0:T(8,128)(2,1)S(1)}, bf16[128,1536]{1,0:T(8,128)(2,1)S(1)}, u32[]{:S(2)}, u32[]{:S(2)}) collective-permute-start(bf16[128,1536]{1,0:T(8,128)(2,1)S(1)} %copy-done.2), channel_id=1, source_target_pairs={{0,3},{1,2},{2,5},{3,4},{4,7},{5,6},{6,1},{7,0},{8,11},{9,10},{10,... | collective-permute-start | bytes 1179656 | tf_op jit(solution)/shard_map/ppermute | solution.py:273
  63.4 46.4 %collective-permute-start.20 = (bf16[128,1536]{1,0:T(8,128)(2,1)S(1)}, bf16[128,1536]{1,0:T(8,128)(2,1)S(1)}, u32[]{:S(2)}, u32[]{:S(2)}) collective-permute-start(bf16[128,1536]{1,0:T(8,128)(2,1)S(1)} %get-tuple-element.27), channel_id=1, source_target_pairs={{0,1},{1,0},{2,3},{3,2},{4,5},{5,4},{6,7},{7,6},{8,9},{9,8},{10,11... | collective-permute-start | bytes 1179656 | tf_op jit(solution)/shard_map/ppermute | solution.py:273
  68.5 35.2 %collective-permute-start.3 = (bf16[128,1536]{1,0:T(8,128)(2,1)S(1)}, bf16[128,1536]{1,0:T(8,128)(2,1)S(1)}, u32[]{:S(2)}, u32[]{:S(2)}) collective-permute-start(bf16[128,1536]{1,0:T(8,128)(2,1)S(1)} %get-tuple-element.30), channel_id=1, source_target_pairs={{0,4},{1,5},{2,6},{3,7},{4,0},{5,1},{6,2},{7,3},{8,12},{9,13},{10,... | collective-permute-start | bytes 1179656 | tf_op jit(solution)/shard_map/ppermute | solution.py:273
  71.8 32.0 %collective-permute-start.4 = (bf16[128,1536]{1,0:T(8,128)(2,1)S(1)}, bf16[128,1536]{1,0:T(8,128)(2,1)S(1)}, u32[]{:S(2)}, u32[]{:S(2)}) collective-permute-start(bf16[128,1536]{1,0:T(8,128)(2,1)S(1)} %get-tuple-element.29), channel_id=1, source_target_pairs={{0,5},{1,4},{2,7},{3,6},{4,1},{5,0},{6,3},{7,2},{8,13},{9,12},{10,... | collective-permute-start | bytes 1179656 | tf_op jit(solution)/shard_map/ppermute | solution.py:273
  75.5 51.0 %collective-permute-start.18 = (bf16[128,1024]{1,0:T(8,128)(2,1)S(1)}, bf16[128,1024]{1,0:T(8,128)(2,1)S(1)}, u32[]{:S(2)}, u32[]{:S(2)}) collective-permute-start(bf16[128,1024]{1,0:T(8,128)(2,1)S(1)} %get-tuple-element.23), channel_id=1, source_target_pairs={{6,0},{7,1},{0,2},{1,3},{2,4},{3,5},{4,6},{5,7},{14,8},{15,9},{8,1... | collective-permute-start | bytes 786440 | tf_op jit(solution)/shard_map/ppermute | solution.py:296
  103.6 18.7 %collective-permute-start.14 = (bf16[128,1024]{1,0:T(8,128)(2,1)S(1)}, bf16[128,1024]{1,0:T(8,128)(2,1)S(1)}, u32[]{:S(2)}, u32[]{:S(2)}) collective-permute-start(bf16[128,1024]{1,0:T(8,128)(2,1)S(1)} %get-tuple-element.21), channel_id=1, source_target_pairs={{2,0},{3,1},{4,2},{5,3},{6,4},{7,5},{0,6},{1,7},{10,8},{11,9},{12,... | collective-permute-start | bytes 786440 | tf_op jit(solution)/shard_map/ppermute | solution.py:296
  106.5 9.4 %collective-permute-start.10 = (bf16[128,1024]{1,0:T(8,128)(2,1)S(1)}, bf16[128,1024]{1,0:T(8,128)(2,1)S(1)}, u32[]{:S(2)}, u32[]{:S(2)}) collective-permute-start(bf16[128,1024]{1,0:T(8,128)(2,1)S(1)} %get-tuple-element.19), channel_id=1, source_target_pairs={{4,0},{5,1},{6,2},{7,3},{0,4},{1,5},{2,6},{3,7},{12,8},{13,9},{14,... | collective-permute-start | bytes 786440 | tf_op jit(solution)/shard_map/ppermute | solution.py:296
  106.6 15.7 %collective-permute-start.11 = (bf16[128,1024]{1,0:T(8,128)(2,1)S(1)}, bf16[128,1024]{1,0:T(8,128)(2,1)S(1)}, u32[]{:S(2)}, u32[]{:S(2)}) collective-permute-start(bf16[128,1024]{1,0:T(8,128)(2,1)S(1)} %get-tuple-element.20), channel_id=1, source_target_pairs={{5,0},{4,1},{7,2},{6,3},{1,4},{0,5},{3,6},{2,7},{13,8},{12,9},{15,... | collective-permute-start | bytes 786440 | tf_op jit(solution)/shard_map/ppermute | solution.py:296
  109.8 16.6 %collective-permute-start.15 = (bf16[128,1024]{1,0:T(8,128)(2,1)S(1)}, bf16[128,1024]{1,0:T(8,128)(2,1)S(1)}, u32[]{:S(2)}, u32[]{:S(2)}) collective-permute-start(bf16[128,1024]{1,0:T(8,128)(2,1)S(1)} %get-tuple-element.22), channel_id=1, source_target_pairs={{3,0},{2,1},{5,2},{4,3},{7,4},{6,5},{1,6},{0,7},{11,8},{10,9},{13,... | collective-permute-start | bytes 786440 | tf_op jit(solution)/shard_map/ppermute | solution.py:296
  115.9 11.7 %collective-permute-start.19 = (bf16[128,1024]{1,0:T(8,128)(2,1)S(1)}, bf16[128,1024]{1,0:T(8,128)(2,1)S(1)}, u32[]{:S(2)}, u32[]{:S(2)}) collective-permute-start(bf16[128,1024]{1,0:T(8,128)(2,1)S(1)} %get-tuple-element.24), channel_id=1, source_target_pairs={{7,0},{6,1},{1,2},{0,3},{3,4},{2,5},{5,6},{4,7},{15,8},{14,9},{9,1... | collective-permute-start | bytes 786440 | tf_op jit(solution)/shard_map/ppermute | solution.py:296
  122.3 5.4 %collective-permute-start.21 = (bf16[128,1024]{1,0:T(8,128)(2,1)S(1)}, bf16[128,1024]{1,0:T(8,128)(2,1)S(1)}, u32[]{:S(2)}, u32[]{:S(2)}) collective-permute-start(bf16[128,1024]{1,0:T(8,128)(2,1)S(1)} %get-tuple-element.26), channel_id=1, source_target_pairs={{1,0},{0,1},{3,2},{2,3},{5,4},{4,5},{7,6},{6,7},{9,8},{8,9},{11,10... | collective-permute-start | bytes 786440 | tf_op jit(solution)/shard_map/ppermute | solution.py:296
  127.6 1.3 %copy-start = (bf16[128,8192]{1,0:T(8,128)(2,1)}, bf16[128,8192]{1,0:T(8,128)(2,1)S(1)}, u32[]{:S(2)}) copy-start(bf16[128,8192]{1,0:T(8,128)(2,1)S(1)} %constant_dynamic-update-slice_fusion.1) | copy-start | bytes 6291460
